TPU v7x, 128 devices: a whole 4x4x4 slice. The times are simulated.
128 devices in a mesh: dp: 8 (over z, y_hi), expert: 4 (over y_lo, core), sample: 4 (over x).
Axes of the slice: x: 4, y: 4 (y_hi: 2, y_lo: 2; y = y_hi * 2 + y_lo), z: 4, core: 2. Of those that a mesh axis runs over, the one named last changes fastest.
Arguments:
- tokens: bfloat16 [2560, 4096], P(('dp', 'expert', 'sample')), may hold values from -6 to 6
- cotangent: bfloat16 [2560, 4096], P(('dp', 'expert', 'sample')), may hold values from -6 to 6
- routes: int32 [2560, 2], P(('dp', 'expert', 'sample')), may hold values from 0 to 7, all different within a row; in each aligned block of 20 rows (0 to 19, 20 to 39, ...) at most 6 rows name the same one
- gate_weights: float32 [2560, 2], P(('dp', 'expert', 'sample')), may hold values from 0.1 to 1
- lengths: int32 [32, 4], P(('dp', 'expert'), 'sample'), may hold values from 1 to 20
- rewards: int32 [32, 4], P(('dp', 'expert'), 'sample'), may hold values from -48 to 48
- w_gate: bfloat16 [8, 8192, 4096], P('expert', ('dp', 'sample')), may hold values from -0.09375 to 0.09375
- w_up: bfloat16 [8, 8192, 4096], P('expert', ('dp', 'sample')), may hold values from -0.09375 to 0.09375
- w_down: bfloat16 [8, 8192, 4096], P('expert', ('dp', 'sample')), may hold values from -0.0625 to 0.0625
Outputs:
- grad_tokens: bfloat16 [2560, 4096], P(('dp', 'expert', 'sample'))
- grad_w_gate: bfloat16 [8, 8192, 4096], P('expert', ('dp', 'sample'))
- grad_w_up: bfloat16 [8, 8192, 4096], P('expert', ('dp', 'sample'))
- grad_w_down: bfloat16 [8, 8192, 4096], P('expert', ('dp', 'sample'))
Inputs may be any that keep to these rules, and one draw needn't show every extreme that they name: `routes`: each row names 2 different experts; among the rows of one device no expert is named by more than 6 rows, and in every draw some device's rows name some expert exactly 6 times.
All inputs are finite; a program needn't handle non-finite values.
Results may differ from a plain program's by a relative error of at most 0.025.
Values may be sent and summed in bfloat16 or wider, within the bound.
A program may use at most 192 MiB of HBM per device.

v0:
```python
import jax
import jax.numpy as jnp
from jax import lax
from jax.sharding import PartitionSpec as P

CAP = 6


def silu_parts(pre_gate):
    gate_prob = jax.nn.sigmoid(pre_gate)
    return (pre_gate * gate_prob, gate_prob * (1.0 + pre_gate * (1.0 - gate_prob)))


def expert_rows(inputs, grads_out, w_gate, w_up, w_down):
    pre_gate = jnp.einsum("rjcd,jfd->rjcf", inputs, w_gate, preferred_element_type=jnp.float32)
    pre_up = jnp.einsum("rjcd,jfd->rjcf", inputs, w_up, preferred_element_type=jnp.float32)
    active, derivative = silu_parts(pre_gate)
    hidden = (active * pre_up).astype(jnp.bfloat16)
    grad_hidden = jnp.einsum(
        "rjcd,jfd->rjcf", grads_out, w_down, preferred_element_type=jnp.float32
    )
    grad_gate = (grad_hidden * pre_up * derivative).astype(jnp.bfloat16)
    grad_up = (grad_hidden * active).astype(jnp.bfloat16)
    return (hidden, grad_gate, grad_up)


def weight_terms(inputs, grads_out, hidden, grad_gate, grad_up):
    term_gate = jnp.einsum("rjcf,rjcd->jfd", grad_gate, inputs, preferred_element_type=jnp.float32)
    term_up = jnp.einsum("rjcf,rjcd->jfd", grad_up, inputs, preferred_element_type=jnp.float32)
    term_down = jnp.einsum("rjcf,rjcd->jfd", hidden, grads_out, preferred_element_type=jnp.float32)
    return (term_gate, term_up, term_down)


def input_terms(grad_gate, grad_up, w_gate, w_up):
    from_gate = jnp.einsum("rjcf,jfd->rjcd", grad_gate, w_gate, preferred_element_type=jnp.float32)
    from_up = jnp.einsum("rjcf,jfd->rjcd", grad_up, w_up, preferred_element_type=jnp.float32)
    return from_gate + from_up


def local(tokens, cotangent, routes, gate_weights, lengths, rewards, w_gate, w_up, w_down):
    samples = lax.axis_size("sample")
    own_reward = rewards.astype(jnp.float32) * 0.0625
    reward_total = lax.psum(own_reward, "sample")
    advantage = own_reward - (reward_total - own_reward) / (samples - 1)
    token_count = tokens.shape[0]
    model_width = tokens.shape[1]
    choices_per = routes.shape[1]
    local_experts = w_gate.shape[0]
    expert_groups = lax.axis_size("expert")
    all_experts = local_experts * expert_groups
    positions = jnp.arange(token_count, dtype=jnp.int32)
    weight_row = jnp.where(positions < lengths[0, 0], -advantage[0, 0], jnp.zeros((), jnp.float32))
    pair_scale = (gate_weights * weight_row[:, None]).reshape(-1)
    pair_expert = routes.reshape(-1)
    member = (pair_expert[:, None] == jnp.arange(all_experts, dtype=jnp.int32)[None, :]).astype(
        jnp.int32
    )
    earlier = jnp.sum((jnp.cumsum(member, axis=0) - member) * member, axis=1)
    target = pair_expert * CAP + earlier
    slot_ids = jnp.arange(all_experts * CAP, dtype=jnp.int32)
    placed = target[:, None] == slot_ids[None, :]
    chosen = jnp.sum(
        placed.reshape(token_count, choices_per, -1).astype(jnp.float32), axis=1
    ).astype(jnp.bfloat16)
    slot_scale = jnp.sum(jnp.where(placed, pair_scale[:, None], jnp.zeros((), jnp.float32)), axis=0)
    sent_inputs = jnp.dot(chosen.T, tokens, preferred_element_type=jnp.float32).astype(jnp.bfloat16)
    sent_cotangent = jnp.dot(chosen.T, cotangent, preferred_element_type=jnp.float32)
    sent_grads = (sent_cotangent * slot_scale[:, None]).astype(jnp.bfloat16)
    layout = (expert_groups, local_experts, CAP, model_width)
    arrived_inputs, arrived_grads = (
        lax.all_to_all(
            sent_inputs.reshape(layout), "expert", split_axis=0, concat_axis=0, tiled=True
        ),
        lax.all_to_all(
            sent_grads.reshape(layout), "expert", split_axis=0, concat_axis=0, tiled=True
        ),
    )
    piece_inputs = lax.all_gather(arrived_inputs, ("dp", "sample"), axis=0, tiled=True)
    piece_grads = lax.all_gather(arrived_grads, ("dp", "sample"), axis=0, tiled=True)
    hidden, grad_gate, grad_up = expert_rows(piece_inputs, piece_grads, w_gate, w_up, w_down)
    add_gate, add_up, add_down = weight_terms(piece_inputs, piece_grads, hidden, grad_gate, grad_up)
    rows_part = input_terms(grad_gate, grad_up, w_gate, w_up)
    partial_value = rows_part
    term_gate, term_up, term_down, partial_value = (add_gate, add_up, add_down, partial_value)
    row_sums = lax.psum_scatter(
        partial_value.astype(jnp.bfloat16), ("dp", "sample"), scatter_dimension=0, tiled=True
    )
    returned = lax.all_to_all(row_sums, "expert", split_axis=0, concat_axis=0, tiled=True)
    flat_back = returned.reshape(all_experts * CAP, model_width)
    grad_tokens = jnp.dot(chosen, flat_back, preferred_element_type=jnp.float32).astype(
        jnp.bfloat16
    )
    return (
        grad_tokens,
        term_gate.astype(jnp.bfloat16),
        term_up.astype(jnp.bfloat16),
        term_down.astype(jnp.bfloat16),
    )


def solution(mesh):
    in_specs = (
        P(("dp", "expert", "sample"), None),
        P(("dp", "expert", "sample"), None),
        P(("dp", "expert", "sample"), None),
        P(("dp", "expert", "sample"), None),
        P(("dp", "expert"), "sample"),
        P(("dp", "expert"), "sample"),
        P("expert", ("dp", "sample"), None),
        P("expert", ("dp", "sample"), None),
        P("expert", ("dp", "sample"), None),
    )
    out_specs = (
        P(("dp", "expert", "sample"), None),
        P("expert", ("dp", "sample"), None),
        P("expert", ("dp", "sample"), None),
        P("expert", ("dp", "sample"), None),
    )
    return jax.shard_map(local, mesh=mesh, in_specs=in_specs, out_specs=out_specs, check_vma=False)
```

profile of v0, /device:TPU:1, one launch (start us, length us, event | category | flops | bytes accessed | tf_op | source)
XLA Modules:
  0.0 764.4 jit_solution(14036604109499341105)
XLA Ops:
  7.2 0.0 copy-start
  7.2 0.0 all-gather.5.cloned.1.call-start
  7.2 0.8 copy.82
  8.0 0.1 eq.35
  8.1 0.1 fusion.37
  8.2 0.1 reduce_window_sum.11
  8.3 0.2 select_reduce_fusion.1
  8.5 0.1 reduce_sum.30
  8.6 0.1 copy.83
  8.6 0.7 multiply_add_fusion
  9.3 0.1 copy.84
  9.4 0.1 fusion.36
  9.5 0.0 copy-done
  9.6 0.3 convolution_convert_fusion
  9.9 0.1 reshape.46
  10.0 0.4 copy.88
  10.4 10.8 %all_to_all.15 = bf16[4,2,6,4096]{3,1,2,0:T(2,128)(2,1)} all-to-all(bf16[4,2,6,4096]{3,1,2,0:T(2,128)(2,1)S(1)} %copy.88), channel_id=1, replica_groups=mesh['dp'=8,'expert'=4,'sample'=4] {'expert'}, dimensions={0} | all-to-all | bytes 786432 | tf_op jit(solution)/shard_map/all_to_all | solution.py:71
  21.2 0.0 all-gather.5.cloned.1.call-update
  21.3 0.0 all-gather.3.cloned.1.call-start
  22.0 9.1 %psum.7 = f32[1,1]{1,0:T(1,128)} all-reduce(f32[1,1]{1,0:T(1,128)S(6)} %mul.63), channel_id=1, replica_groups=mesh['dp'=8,'expert'=4,'sample'=4] {'sample'}, use_global_device_ids=true, to_apply=%region_3.4 | all-reduce | flops 1 | bytes 8 | tf_op jit(solution)/shard_map/psum | solution.py:43
  32.4 0.7 broadcast_multiply_fusion
  33.0 0.1 copy.85
  33.1 0.1 broadcast_in_dim.29
  33.3 0.1 select_reduce_fusion
  33.3 1.2 fusion.19
  34.6 0.1 reshape.45
  34.7 0.4 copy.86
  35.1 12.8 %all_to_all.16 = bf16[4,2,6,4096]{3,1,2,0:T(2,128)(2,1)} all-to-all(bf16[4,2,6,4096]{3,1,2,0:T(2,128)(2,1)S(1)} %copy.86), channel_id=1, replica_groups=mesh['dp'=8,'expert'=4,'sample'=4] {'expert'}, dimensions={0} | all-to-all | bytes 786432 | tf_op jit(solution)/shard_map/all_to_all | solution.py:74
  47.9 0.0 all-gather.3.cloned.1.call-update
  48.0 0.3 all-reduce.3.cloned.1.call-start
  48.2 104.0 %all-gather.5.cloned.1.call-done = bf16[128,2,6,4096]{3,1,2,0:T(2,128)(2,1)} async-done(((bf16[4,2,6,4096]{3,1,2,0:T(2,128)(2,1)}), bf16[128,2,6,4096]{3,1,2,0:T(2,128)(2,1)}) %all-gather.5.cloned.1.call-update) | async-done | bytes 12582928 | tf_op jit(solution)/shard_map/all_gather | solution.py:78
  152.2 0.0 copy-start.2
  152.2 14.3 %fusion.9 = f32[2,128,6,256]{3,1,2,0:T(8,128)} fusion(bf16[128,2,6,4096]{3,1,2,0:T(2,128)(2,1)} %all-gather.5.cloned.1.call-done, bf16[2,256,4096]{2,1,0:T(8,128)(2,1)} %param.15), kind=kOutput, calls=%fused_computation.13 | convolution fusion | flops 3221225472 | bytes 18350080 | tf_op jit(solution)/shard_map/rjcd,jfd->rjcf/dot_general | solution.py:15
  166.5 0.0 copy-done.2
  166.5 13.5 %fusion.11 = f32[2,128,6,256]{3,1,2,0:T(8,128)} fusion(bf16[128,2,6,4096]{3,1,2,0:T(2,128)(2,1)} %all-gather.5.cloned.1.call-done, bf16[2,256,4096]{2,1,0:T(8,128)(2,1)S(1)} %copy-done.2), kind=kOutput, calls=%fused_computation.15 | convolution fusion | flops 3221225472 | bytes 18350080 | tf_op jit(solution)/shard_map/rjcd,jfd->rjcf/dot_general | solution.py:16
  180.0 101.6 %all-gather.3.cloned.1.call-done = bf16[128,2,6,4096]{3,1,2,0:T(2,128)(2,1)} async-done(((bf16[4,2,6,4096]{3,1,2,0:T(2,128)(2,1)}), bf16[128,2,6,4096]{3,1,2,0:T(2,128)(2,1)}) %all-gather.3.cloned.1.call-update) | async-done | bytes 12582928 | tf_op jit(solution)/shard_map/all_gather | solution.py:79
  281.6 14.4 %fusion.34 = (bf16[128,2,6,256]{3,0,2,1:T(8,128)(2,1)S(1)}, bf16[128,2,6,256]{3,0,2,1:T(8,128)(2,1)S(1)}) fusion(f32[2,128,6,256]{3,1,2,0:T(8,128)} %fusion.9, f32[2,128,6,256]{3,1,2,0:T(8,128)} %fusion.11, bf16[2,256,4096]{2,1,0:T(8,128)(2,1)} %param.17, bf16[128,2,6,4096]{3,1,2,0:T(2,128)(2,1)} %all-gather.3.cloned.1.call-done), kind=kOutput, calls=%fused_computation.41 | convolution fusion | flops 3226337280 | bytes 21495808 | tf_op jit(solution)/shard_map/rjcd,jfd->rjcf/dot_general | solution.py:19
  296.0 12.3 %fusion.20 = f32[2,128,6,4096]{3,1,2,0:T(8,128)} fusion(bf16[128,2,6,256]{3,0,2,1:T(8,128)(2,1)S(1)} %get-tuple-element.5, bf16[2,256,4096]{2,1,0:T(8,128)(2,1)} %param.15), kind=kOutput, calls=%fused_computation.21 | convolution fusion | flops 3221225472 | bytes 30146560 | tf_op jit(solution)/shard_map/rjcf,jfd->rjcd/dot_general | solution.py:35
  308.3 15.5 %fusion = bf16[128,2,6,4096]{3,0,2,1:T(8,128)(2,1)} fusion(f32[2,128,6,4096]{3,1,2,0:T(8,128)} %fusion.20, bf16[128,2,6,256]{3,0,2,1:T(8,128)(2,1)S(1)} %get-tuple-element.4, bf16[2,256,4096]{2,1,0:T(8,128)(2,1)} %param.16), kind=kOutput, calls=%fused_computation.1 | convolution fusion | flops 3233808384 | bytes 42729472 | tf_op jit(solution)/shard_map/rjcf,jfd->rjcd/dot_general | solution.py:36
  323.8 0.0 copy-start.3
  323.8 0.0 all-reduce.3.cloned.1.call-update
  323.9 0.6 copy-done.3
  324.5 0.6 dynamic-slice
  325.7 0.0 copy-start.4
  325.7 0.0 copy-start.5
  325.7 22.0 %bitcast_convert_fusion.1 = bf16[2,256,4096]{2,1,0:T(8,128)(2,1)} fusion(bf16[128,2,6,256]{3,0,2,1:T(8,128)(2,1)S(1)} %get-tuple-element.4, bf16[128,2,6,4096]{3,1,2,0:T(2,128)(2,1)} %all-gather.5.cloned.1.call-done), kind=kOutput, calls=%fused_computation.7 | convolution fusion | flops 3223322624 | bytes 17563648 | tf_op jit(solution)/shard_map/rjcf,rjcd->jfd/dot_general | solution.py:29
  347.7 0.0 copy-done.4
  347.7 0.0 copy-done.5
  347.7 22.4 %bitcast_convert_fusion = bf16[2,256,4096]{2,1,0:T(8,128)(2,1)} fusion(bf16[128,2,6,4096]{3,1,2,0:T(2,128)(2,1)} %all-gather.3.cloned.1.call-done, f32[2,128,6,256]{3,1,2,0:T(8,128)S(1)} %copy-done.5, f32[2,128,6,256]{3,1,2,0:T(8,128)S(1)} %copy-done.4), kind=kOutput, calls=%fused_computation.6 | convolution fusion | flops 3225681920 | bytes 19922944 | tf_op jit(solution)/shard_map/rjcf,rjcd->jfd/dot_general | solution.py:30
  370.1 339.8 %all-reduce.3.cloned.1.call-done = bf16[128,2,6,4096]{3,0,2,1:T(8,128)(2,1)} async-done(((bf16[128,2,6,4096]{3,0,2,1:T(8,128)(2,1)}), bf16[128,2,6,4096]{3,0,2,1:T(8,128)(2,1)}) %all-reduce.3.cloned.1.call-update) | async-done | bytes 12582928
  709.9 1.4 constant_dynamic-slice_fusion
  711.3 1.1 copy.91
  712.4 22.1 %all-to-all-start.2 = ((bf16[4,2,6,4096]{3,1,2,0:T(2,128)(2,1)}), bf16[4,2,6,4096]{3,1,2,0:T(2,128)(2,1)S(1)}, u32[]{:S(2)}, u32[]{:S(2)}) async-start(bf16[4,2,6,4096]{3,1,2,0:T(2,128)(2,1)} %copy.91), calls=%async_computation.2 | async-start | bytes 786432 | tf_op jit(solution)/shard_map/all_to_all | solution.py:88
  734.5 0.0 copy-start.1
  734.6 21.9 %bitcast_convert_fusion.2 = bf16[2,256,4096]{2,1,0:T(8,128)(2,1)} fusion(bf16[128,2,6,256]{3,0,2,1:T(8,128)(2,1)S(1)} %get-tuple-element.5, bf16[128,2,6,4096]{3,1,2,0:T(2,128)(2,1)} %all-gather.5.cloned.1.call-done), kind=kOutput, calls=%fused_computation.8 | convolution fusion | flops 3223322624 | bytes 17563648 | tf_op jit(solution)/shard_map/rjcf,rjcd->jfd/dot_general | solution.py:28
  756.4 0.0 all-to-all-done.2
  756.4 0.2 copy.92
  756.7 0.1 reshape.47
  756.8 0.9 convolution_convert_fusion.1
  757.7 0.0 copy-done.1
  (2 shorter events, 0.0 us)
Async XLA Ops:
  7.2 2.4 copy-start
  7.2 145.0 %all-gather.5.cloned.1.call-start = ((), (), s32[]{:S(2)}) async-start(), calls=%async_computation.4 | async-start | bytes 12976128 | tf_op jit(solution)/shard_map/all_gather | solution.py:78
  21.3 260.3 %all-gather.3.cloned.1.call-start = ((), (), s32[]{:S(2)}) async-start(), calls=%async_computation.3 | async-start | bytes 12976128 | tf_op jit(solution)/shard_map/all_gather | solution.py:79
  48.0 662.0 %all-reduce.3.cloned.1.call-start = ((), (), s32[]{:S(2)}) async-start(), calls=%async_computation.5 | async-start | bytes 25165824
  152.2 14.3 %copy-start.2 = (bf16[2,256,4096]{2,1,0:T(8,128)(2,1)S(1)}, bf16[2,256,4096]{2,1,0:T(8,128)(2,1)}, u32[]{:S(2)}) copy-start(bf16[2,256,4096]{2,1,0:T(8,128)(2,1)} %param.16) | copy-start | bytes 12582916
  323.8 0.7 copy-start.3
  325.7 22.0 %copy-start.4 = (f32[2,128,6,256]{3,1,2,0:T(8,128)S(1)}, f32[2,128,6,256]{3,1,2,0:T(8,128)}, u32[]{:S(2)}) copy-start(f32[2,128,6,256]{3,1,2,0:T(8,128)} %fusion.9) | copy-start | bytes 4718596
  325.7 22.0 %copy-start.5 = (f32[2,128,6,256]{3,1,2,0:T(8,128)S(1)}, f32[2,128,6,256]{3,1,2,0:T(8,128)}, u32[]{:S(2)}) copy-start(f32[2,128,6,256]{3,1,2,0:T(8,128)} %fusion.11) | copy-start | bytes 4718596
  712.4 44.0 %all-to-all-start.2 = ((bf16[4,2,6,4096]{3,1,2,0:T(2,128)(2,1)}), bf16[4,2,6,4096]{3,1,2,0:T(2,128)(2,1)S(1)}, u32[]{:S(2)}, u32[]{:S(2)}) async-start(bf16[4,2,6,4096]{3,1,2,0:T(2,128)(2,1)} %copy.91), calls=%async_computation.2 | async-start | bytes 786432 | tf_op jit(solution)/shard_map/all_to_all | solution.py:88
  734.5 23.1 %copy-start.1 = (bf16[20,4096]{1,0:T(8,128)(2,1)S(1)}, bf16[20,4096]{1,0:T(8,128)(2,1)}, u32[]{:S(2)}) copy-start(bf16[20,4096]{1,0:T(8,128)(2,1)} %param.9) | copy-start | bytes 491524
Sparse Core Ops, SparseCore 0:
  21.4 130.7 all-gather.4
  155.2 126.3 all-gather.2
  324.0 385.9 all-reduce.2
where the time goes:
time: 768 us; the launch traced here: 764 us
  waiting for transfers between devices  545 us (71%)
  matrix products  139 us (18%)
  blocking collectives  32.7 us (4%)
  starting transfers between devices  22.4 us (3%)
  between operations  16.8 us (2%)
    unnamed x4, waiting for transfers between devices  340 us
    all_gather x1, waiting for transfers between devices, local(): lax.all_gather(arrived_inputs, ('dp', 'sample'), axis=0, tiled=True)  104 us
    all_gather x1, waiting for transfers between devices, local(): lax.all_gather(arrived_grads, ('dp', 'sample'), axis=0, tiled=True)  102 us
    dot_general x1, matrix products, weight_terms(): jnp.einsum('rjcf,rjcd->jfd', hidden, grads_out, preferred_element_type=jn...  22.4 us
    all_to_all x1, starting transfers between devices, local(): lax.all_to_all(row_sums, 'expert', split_axis=0, concat_axis=0, tiled=True)  22.1 us
    dot_general x1, matrix products, weight_terms(): jnp.einsum('rjcf,rjcd->jfd', grad_up, inputs, preferred_element_type=jnp....  22 us
    dot_general x1, matrix products, weight_terms(): jnp.einsum('rjcf,rjcd->jfd', grad_gate, inputs, preferred_element_type=jn...  21.9 us
    dot_general x1, matrix products, input_terms(): jnp.einsum('rjcf,jfd->rjcd', grad_up, w_up, preferred_element_type=jnp.fl...  15.5 us
  transfers between devices with their start and end apart: 4, of which 3 were waited for; matrix products, arithmetic and copies ran while one was open for 13% of the time, Pallas kernels for 0%

commit v1 on v0

v1 whole, which is shorter than its diff:
```python
import functools

import jax
import jax.numpy as jnp
from jax import lax
from jax.experimental import pallas as pl
from jax.experimental.pallas import tpu as pltpu
from jax.sharding import PartitionSpec as P

CAP = 6
RING = 4
WIDTH = 4096
META = 128
ROWS = 40
MESH = pl.DeviceIdType.MESH
ORDERS = (("x", "y", "z"), ("y", "z", "x"), ("z", "x", "y"))
BF = jnp.bfloat16
F32 = jnp.float32


def place():
    dp = lax.axis_index("dp")
    ex = lax.axis_index("expert")
    return {"x": lax.axis_index("sample"), "y": (dp % 2) * 2 + ex // 2, "z": dp // 2}, ex % 2


def device(at, core):
    return {
        "dp": at["z"] * 2 + at["y"] // 2,
        "expert": (at["y"] % 2) * 2 + core,
        "sample": at["x"],
    }


def moved(at, axis, by):
    return {**at, axis: lax.rem(at[axis] + (by + RING), RING)}


def greet(at, core):
    barrier = pltpu.get_barrier_semaphore()
    peers = [device(moved(at, axis, by), core) for axis in "xyz" for by in (1, -1)]
    peers.append(device(at, 1 - core))
    for peer in peers:
        pl.semaphore_signal(barrier, inc=1, device_id=peer, device_id_type=MESH)
    pl.semaphore_wait(barrier, len(peers))


def remote(src, dst, send, recv, peer):
    return pltpu.make_async_remote_copy(
        src_ref=src, dst_ref=dst, send_sem=send, recv_sem=recv, device_id=peer, device_id_type=MESH
    )


GATHER_COPIES = 35


def gather_kernel(own_ref, out_ref, mate, block, send, recv, keep):
    at, core = place()
    partner = device(at, 1 - core)
    greet(at, core)
    swap = remote(own_ref.at[1 - core], mate, send.at[3, 0], recv.at[3, 0], partner)
    swap.start()
    swap.wait()

    @pl.when(core == 0)
    def _():
        block[0:20] = own_ref[0]
        block[20:40] = mate[...]

    @pl.when(core == 1)
    def _():
        block[0:20] = mate[...]
        block[20:40] = own_ref[1]

    here = pltpu.make_async_copy(block, out_ref.at[core, at["z"], at["y"], at["x"]], keep)
    here.start()
    part = (WIDTH + META) // 3
    copies = {}

    def view(p, **over):
        to = {**at, **over}
        return out_ref.at[core, to["z"], to["y"], to["x"], :, pl.ds(p * part, part)]

    def push(p, k, src, dst, peer):
        copy = remote(src, dst, send.at[p, k], recv.at[p, k], peer)
        copy.start()
        copies[p, k] = copy

    def hand(p, k, ref):
        push(p, k, ref, ref, partner)

    def near(axis, by):
        return device(moved(at, axis, by), core)

    def coord(axis, by):
        return at[axis] if by == 0 else moved(at, axis, by)[axis]

    every = pl.ds(0, RING)
    offset = (0, -1, 1, 2)

    def line(p, l, plane=0):
        d1, d2, d3 = ORDERS[p]
        return view(p, **{d1: every, d2: coord(d2, offset[l]), d3: coord(d3, plane)})

    def spread(p, l):
        d3 = ORDERS[p][2]
        for k, by in enumerate((1, -1)):
            push(p, 7 + 2 * l + k, line(p, l), line(p, l), near(d3, by))
        hand(p, 19 + l, line(p, l))

    for p, (d1, d2, d3) in enumerate(ORDERS):
        mine = block.at[:, pl.ds(p * part, part)]
        push(p, 0, mine, view(p), near(d1, 1))
        push(p, 1, mine, view(p), near(d1, -1))
    for p, (d1, d2, d3) in enumerate(ORDERS):
        copies[p, 0].wait_recv()
        got = view(p, **{d1: coord(d1, -1)})
        push(p, 2, got, got, near(d1, 1))
    here.wait()
    for p, (d1, d2, d3) in enumerate(ORDERS):
        copies[p, 1].wait_recv()
        copies[p, 2].wait_recv()
        push(p, 3, line(p, 0), line(p, 0), near(d2, 1))
        push(p, 4, line(p, 0), line(p, 0), near(d2, -1))
    for p in range(3):
        spread(p, 0)
    for p, (d1, d2, d3) in enumerate(ORDERS):
        copies[p, 3].wait_recv()
        got = view(p, **{d1: pl.ds(0, 2), d2: coord(d2, -1)})
        push(p, 5, got, got, near(d2, 1))
        copies[p, 4].wait_recv()
        got = view(p, **{d1: pl.ds(2, 2), d2: coord(d2, 1)})
        push(p, 6, got, got, near(d2, -1))
    for p in range(3):
        spread(p, 1)
        spread(p, 2)

    def arrived(p, l):
        d3 = ORDERS[p][2]
        for k, by in enumerate((1, -1)):
            copies[p, 7 + 2 * l + k].wait_recv()
            got = line(p, l, -by)
            if k == l // 2:
                push(p, 15 + l, got, got, near(d3, by))
            hand(p, 23 + 4 * k + l, got)

    for p in range(3):
        arrived(p, 0)
    for p in range(3):
        copies[p, 5].wait_recv()
        copies[p, 6].wait_recv()
        spread(p, 3)
    for l in (1, 2, 3):
        for p in range(3):
            arrived(p, l)
    for l in range(4):
        for p in range(3):
            copies[p, 15 + l].wait_recv()
            hand(p, 31 + l, line(p, l, 2))
    for p in range(3):
        for k in range(19, GATHER_COPIES):
            copies[p, k].wait_recv()
    for copy in copies.values():
        copy.wait_send()


def gather_rows(own):
    return pl.pallas_call(
        gather_kernel,
        out_shape=jax.ShapeDtypeStruct((2, RING, RING, RING, ROWS, WIDTH + META), BF),
        in_specs=[pl.BlockSpec(memory_space=pltpu.VMEM)],
        out_specs=pl.BlockSpec(memory_space=pl.ANY),
        scratch_shapes=[
            pltpu.VMEM((ROWS // 2, WIDTH + META), BF),
            pltpu.VMEM((ROWS, WIDTH + META), BF),
            pltpu.SemaphoreType.DMA((4, GATHER_COPIES)),
            pltpu.SemaphoreType.DMA((4, GATHER_COPIES)),
            pltpu.SemaphoreType.DMA,
        ],
        compiler_params=pltpu.CompilerParams(collective_id=0, has_side_effects=True),
        name="gather_rows",
    )(own)


HALF = WIDTH // 2
WIDTHS = (768, 640, 640)
STARTS = (0, 768, 1408)
AHEAD = (3, 1)
BEHIND = (2, 0)


def scatter_kernel(p_ref, out_ref, *scratch):
    acc, mate, fa, ma, pa, fb, mb, pb, fc, mc, pc = [scratch[3 * i : 3 * i + 3] for i in range(11)]
    done, other_done, load, load_far, far_in, send, recv = scratch[33:]
    at, core = place()
    partner = device(at, 1 - core)
    greet(at, core)
    copies = {}
    every = pl.ds(0, RING)
    offset = (0, -1, 1, 2)

    def near(axis, by):
        return device(moved(at, axis, by), core)

    def coord(axis, by):
        return at[axis] if by == 0 else moved(at, axis, by)[axis]

    def spot(**over):
        to = {**at, **over}
        return to["z"], to["y"], to["x"]

    def plane_at(p, by):
        d1, d2, d3 = ORDERS[p]
        return spot(**{d1: every, d2: every, d3: coord(d3, by)})

    def columns(p, side):
        return pl.ds(pl.multiple_of(side * HALF + STARTS[p], 128), WIDTHS[p])

    def push(p, key, k, src, dst, peer):
        copy = remote(src, dst, send.at[p, k], recv.at[p, k], peer)
        copy.start()
        copies[(p,) + key] = copy

    loads = {}
    for n, by in enumerate((2, 1, -1, 0)):
        for p in range(3):
            where = plane_at(p, by)
            far = remote(
                p_ref.at[where + (slice(None), columns(p, 1 - core))],
                mate[p].at[where],
                load_far.at[p, n],
                far_in.at[p, n],
                partner,
            )
            far.start()
            own = pltpu.make_async_copy(
                p_ref.at[where + (slice(None), columns(p, core))], acc[p].at[where], load.at[p, n]
            )
            own.start()
            loads[p, by] = (own, far)

    def add(dst, index, *terms):
        total = dst[index].astype(F32)
        for ref, where in terms:
            total = total + ref[where].astype(F32)
        dst[index] = total.astype(BF)

    def ready(p, by):
        own, far = loads[p, by]
        own.wait()
        far.wait_recv()
        d1, d2, d3 = ORDERS[p]

        def body(i, carry):
            where = spot(**{d1: i % RING, d2: i // RING, d3: coord(d3, by)})
            add(acc[p], where, (mate[p], where))
            return carry

        lax.fori_loop(0, RING * RING, body, 0)

    def line(p, r, by):
        d1, d2, d3 = ORDERS[p]
        return acc[p].at[spot(**{d1: every, d2: coord(d2, offset[r]), d3: coord(d3, by)})]

    def add_line(p, r, by, *terms, first=0, count=RING):
        d1, d2, d3 = ORDERS[p]

        def body(i, carry):
            where = spot(**{d1: i, d2: coord(d2, offset[r]), d3: coord(d3, by)})
            add(acc[p], where, *[(ref, (r, i) if lead else (i,)) for ref, lead in terms])
            return carry

        lax.fori_loop(first, first + count, body, 0)

    for p in range(3):
        ready(p, 2)
        for r in (3, 2, 1, 0):
            push(p, ("fa", r), r, line(p, r, 2), fa[p].at[r], near(ORDERS[p][2], 1 if r in AHEAD else -1))
    for p in range(3):
        ready(p, 1)
        for r in BEHIND:
            push(p, ("ma", r), 4 + r, line(p, r, 1), ma[p].at[r], near(ORDERS[p][2], 1))
    for p in range(3):
        ready(p, -1)
        for r in AHEAD:
            push(p, ("pa", r), 8 + r, line(p, r, -1), pa[p].at[r], near(ORDERS[p][2], -1))
    for p in range(3):
        ready(p, 0)
    for r in (3, 2, 1, 0):
        for p in range(3):
            copies[p, "fa", r].wait_recv()
            if r in AHEAD:
                add_line(p, r, 1, (fa[p], True))
                push(p, ("ma", r), 4 + r, line(p, r, 1), ma[p].at[r], near(ORDERS[p][2], 1))
            else:
                add_line(p, r, -1, (fa[p], True))
                push(p, ("pa", r), 8 + r, line(p, r, -1), pa[p].at[r], near(ORDERS[p][2], -1))

    def piece(p, r, half):
        d1, d2, d3 = ORDERS[p]
        return acc[p].at[spot(**{d1: pl.ds(2 * half, 2), d2: coord(d2, offset[r])})]

    def half_of(ref, half):
        return ref.at[pl.ds(2 * half, 2)]

    for r in (3, 2, 1, 0):
        for p in range(3):
            copies[p, "ma", r].wait_recv()
            copies[p, "pa", r].wait_recv()
            add_line(p, r, 0, (ma[p], True), (pa[p], True))
            d2 = ORDERS[p][1]
            if r == 3:
                push(p, ("fb", 0), 12, piece(p, 3, 0), half_of(fb[p], 0), near(d2, 1))
                push(p, ("fb", 1), 13, piece(p, 3, 1), half_of(fb[p], 1), near(d2, -1))
            if r == 2:
                push(p, ("mb", 1), 15, piece(p, 2, 1), half_of(mb[p], 1), near(d2, 1))
            if r == 1:
                push(p, ("pb", 0), 16, piece(p, 1, 0), half_of(pb[p], 0), near(d2, -1))
    for p in range(3):
        d2 = ORDERS[p][1]
        copies[p, "fb", 0].wait_recv()
        add_line(p, 2, 0, (fb[p], False), first=0, count=2)
        push(p, ("mb", 0), 14, piece(p, 2, 0), half_of(mb[p], 0), near(d2, 1))
        copies[p, "fb", 1].wait_recv()
        add_line(p, 1, 0, (fb[p], False), first=2, count=2)
        push(p, ("pb", 1), 17, piece(p, 1, 1), half_of(pb[p], 1), near(d2, -1))

    def cell(p, by):
        d1 = ORDERS[p][0]
        return spot(**{d1: coord(d1, by)})

    for p in range(3):
        d1 = ORDERS[p][0]
        for half in (0, 1):
            copies[p, "mb", half].wait_recv()
            copies[p, "pb", half].wait_recv()
        add_line(p, 0, 0, (mb[p], False), (pb[p], False))
        push(p, ("fc",), 18, acc[p].at[cell(p, 2)], fc[p], near(d1, 1))
        push(p, ("pc",), 20, acc[p].at[cell(p, -1)], pc[p], near(d1, -1))
    for p in range(3):
        d1 = ORDERS[p][0]
        copies[p, "fc"].wait_recv()
        add(acc[p], cell(p, 1), (fc[p], ...))
        push(p, ("mc",), 19, acc[p].at[cell(p, 1)], mc[p], near(d1, 1))
    for p in range(3):
        copies[p, "pc"].wait_recv()
        copies[p, "mc"].wait_recv()
        own = acc[p][cell(p, 0)].astype(F32) + pc[p][...].astype(F32) + mc[p][...].astype(F32)
        done[:, STARTS[p] : STARTS[p] + WIDTHS[p]] = own.astype(BF)
    last = remote(done, other_done, send.at[3, 0], recv.at[3, 0], partner)
    last.start()
    last.wait_recv()

    @pl.when(core == 0)
    def _():
        out_ref[:, :HALF] = done[0:20]
        out_ref[:, HALF:] = other_done[0:20]

    @pl.when(core == 1)
    def _():
        out_ref[:, :HALF] = other_done[20:40]
        out_ref[:, HALF:] = done[20:40]

    last.wait_send()
    for copy in copies.values():
        copy.wait_send()
    for _, far in loads.values():
        far.wait_send()


def scatter_sum(partial):
    full = [pltpu.VMEM((RING, RING, RING, ROWS, w), BF) for w in WIDTHS]
    lines = [pltpu.VMEM((RING, RING, ROWS, w), BF) for w in WIDTHS]
    line = [pltpu.VMEM((RING, ROWS, w), BF) for w in WIDTHS]
    cell = [pltpu.VMEM((ROWS, w), BF) for w in WIDTHS]
    return pl.pallas_call(
        scatter_kernel,
        out_shape=jax.ShapeDtypeStruct((ROWS // 2, WIDTH), BF),
        in_specs=[pl.BlockSpec(memory_space=pl.ANY)],
        out_specs=pl.BlockSpec(memory_space=pltpu.VMEM),
        scratch_shapes=full * 2
        + lines * 3
        + line * 3
        + cell * 3
        + [pltpu.VMEM((ROWS, HALF), BF)] * 2
        + [pltpu.SemaphoreType.DMA((3, 4))] * 3
        + [pltpu.SemaphoreType.DMA((4, 21))] * 2,
        compiler_params=pltpu.CompilerParams(
            collective_id=1, has_side_effects=True, vmem_limit_bytes=60 * 1024 * 1024
        ),
        name="scatter_sum",
    )(partial)


GROUP = 160
SLOTS = 48


def turned(a, b):
    return lax.dot_general(a, b, (((0,), (0,)), ((), ())), preferred_element_type=F32)


def select_kernel(group_ref, all_ref, x_ref, g_ref, pick_ref):
    info = all_ref[0, 0, :, WIDTH:]
    meta = info.astype(F32)
    row = lax.broadcasted_iota(jnp.int32, (GROUP, 1), 0)
    lane = lax.broadcasted_iota(jnp.int32, (GROUP, 128), 1)
    same = lax.broadcasted_iota(jnp.int32, (GROUP, GROUP), 0) % ROWS == (
        lax.broadcasted_iota(jnp.int32, (GROUP, GROUP), 1) % ROWS
    )
    total = jnp.dot(same.astype(F32).astype(BF), info, preferred_element_type=F32)[:, 9:10] * 0.0625
    reward = meta[:, 9:10] * 0.0625
    advantage = reward - (total - reward) / 3.0
    live = (row % 20).astype(F32) < meta[:, 8:9]
    weight = jnp.where(live, -advantage, 0.0)
    first = (2 * group_ref[0]).astype(F32)
    scale = jnp.zeros((128, 128), F32)
    pick = jnp.zeros((GROUP, 128), F32)
    for k in range(2):
        j = meta[:, k : k + 1] - first
        valid = (j >= 0.0) & (j < 2.0)
        slot = j * SLOTS + ((row // 20) * CAP).astype(F32) + meta[:, 10 + k : 11 + k]
        slot = jnp.where(valid, slot, -1.0).astype(jnp.int32)
        one = (lane == slot).astype(F32)
        pick = pick + one
        c = 2 + 3 * k
        value = ((meta[:, c : c + 1] + meta[:, c + 1 : c + 2]) + meta[:, c + 2 : c + 3]) * weight
        high = value.astype(BF).astype(F32)
        middle = (value - high).astype(BF).astype(F32)
        low = value - high - middle
        pieces = jnp.where(lane == 0, high, jnp.where(lane == 1, middle, jnp.where(lane == 2, low, 0.0)))
        scale = scale + turned(one.astype(BF), pieces.astype(BF))
    column = (scale[:, 0:1] + scale[:, 1:2]) + scale[:, 2:3]
    pick = pick.astype(BF)
    pick_ref[0] = pick
    for start in range(0, WIDTH, 1024):
        cols = slice(start, start + 1024)
        x = turned(pick, all_ref[0, 0, :, cols]).astype(BF)
        g = (turned(pick, all_ref[1, 0, :, cols]) * column).astype(BF)
        for j in range(2):
            x_ref[j, :, cols] = x[j * SLOTS : (j + 1) * SLOTS]
            g_ref[j, :, cols] = g[j * SLOTS : (j + 1) * SLOTS]


def select_rows(group, everything):
    blocks = everything.shape[1]
    rows = jax.ShapeDtypeStruct((2, blocks * SLOTS, WIDTH), BF)
    return pl.pallas_call(
        select_kernel,
        grid=(blocks,),
        out_shape=(rows, rows, jax.ShapeDtypeStruct((blocks, GROUP, 128), BF)),
        in_specs=[
            pl.BlockSpec(memory_space=pltpu.SMEM),
            pl.BlockSpec((2, 1, GROUP, WIDTH + META), lambda b: (0, b, 0, 0)),
        ],
        out_specs=(
            pl.BlockSpec((2, SLOTS, WIDTH), lambda b: (0, b, 0)),
            pl.BlockSpec((2, SLOTS, WIDTH), lambda b: (0, b, 0)),
            pl.BlockSpec((1, GROUP, 128), lambda b: (b, 0, 0)),
        ),
        name="select_rows",
    )(group, everything)


def combine_kernel(pick_ref, r_ref, out_ref):
    for start in range(0, WIDTH, 1024):
        cols = slice(start, start + 1024)
        total = jnp.dot(pick_ref[0, :, :SLOTS], r_ref[0, :, cols], preferred_element_type=F32)
        total += jnp.dot(pick_ref[0, :, SLOTS : 2 * SLOTS], r_ref[1, :, cols], preferred_element_type=F32)
        out_ref[0, :, cols] = total.astype(BF)


def combine_rows(pick, rows):
    blocks = pick.shape[0]
    return pl.pallas_call(
        combine_kernel,
        grid=(blocks,),
        out_shape=jax.ShapeDtypeStruct((blocks, GROUP, WIDTH), BF),
        in_specs=[
            pl.BlockSpec((1, GROUP, 128), lambda b: (b, 0, 0)),
            pl.BlockSpec((2, SLOTS, WIDTH), lambda b: (0, b, 0)),
        ],
        out_specs=pl.BlockSpec((1, GROUP, WIDTH), lambda b: (b, 0, 0)),
        name="combine_rows",
    )(pick, rows)


def three(values):
    high = lax.reduce_precision(values, 8, 7)
    middle = lax.reduce_precision(values - high, 8, 7)
    return [high, middle, values - high - middle]


def own_rows(tokens, cotangent, routes, gate_weights, lengths, rewards):
    count = tokens.shape[0]
    flat = routes.reshape(-1)
    before = jnp.arange(2 * count)[:, None] > jnp.arange(2 * count)[None, :]
    same = flat[:, None] == flat[None, :]
    earlier = jnp.sum((before & same).astype(jnp.int32), axis=1).reshape(count, 2)
    wide = jnp.ones((count, 1), F32)
    columns = [routes.astype(F32)]
    for k in range(2):
        columns += three(gate_weights[:, k : k + 1])
    columns += [wide * lengths[0, 0].astype(F32), wide * rewards[0, 0].astype(F32), earlier.astype(F32)]
    meta = jnp.concatenate(columns, axis=1)
    meta = jnp.pad(meta, ((0, 0), (0, META - meta.shape[1]))).astype(BF)
    return jnp.stack(
        [jnp.concatenate([tokens, meta], axis=1), jnp.concatenate([cotangent, jnp.zeros_like(meta)], axis=1)]
    )


def local(tokens, cotangent, routes, gate_weights, lengths, rewards, w_gate, w_up, w_down):
    own = own_rows(tokens, cotangent, routes, gate_weights, lengths, rewards)
    everything = gather_rows(own)
    everything = everything.reshape(2, RING * RING, GROUP, WIDTH + META)
    group = lax.axis_index("expert").astype(jnp.int32).reshape(1)
    x, g, pick = select_rows(group, everything)
    forward = functools.partial(jnp.einsum, "jcd,jfd->jcf", preferred_element_type=F32)
    back = functools.partial(jnp.einsum, "jcf,jfd->jcd", preferred_element_type=F32)
    weigh = functools.partial(jnp.einsum, "jcf,jcd->jfd", preferred_element_type=F32)
    pre_gate, pre_up, grad_hidden = forward(x, w_gate), forward(x, w_up), forward(g, w_down)
    prob = jax.nn.sigmoid(pre_gate)
    active = pre_gate * prob
    hidden = (active * pre_up).astype(BF)
    grad_gate = (grad_hidden * pre_up * (prob * (1.0 + pre_gate * (1.0 - prob)))).astype(BF)
    grad_up = (grad_hidden * active).astype(BF)
    rows = (back(grad_gate, w_gate) + back(grad_up, w_up)).astype(BF)
    partial = combine_rows(pick, rows).reshape(RING, RING, RING, ROWS, WIDTH)
    grad_tokens = scatter_sum(partial)
    return (
        grad_tokens,
        weigh(grad_gate, x).astype(BF),
        weigh(grad_up, x).astype(BF),
        weigh(hidden, g).astype(BF),
    )


def solution(mesh):
    rows = P(("dp", "expert", "sample"), None)
    pair = P(("dp", "expert"), "sample")
    weights = P("expert", ("dp", "sample"), None)
    return jax.shard_map(
        local,
        mesh=mesh,
        in_specs=(rows,) * 4 + (pair,) * 2 + (weights,) * 3,
        out_specs=(rows,) + (weights,) * 3,
        check_vma=False,
    )
```

time: 768 us -> 304 us (0.40)
  waiting for transfers between devices: 545 us -> 0 us
  Pallas kernels: 0 us -> 217 us
  matrix products: 139 us -> 77.1 us
  blocking collectives: 32.7 us -> 0 us
  starting transfers between devices: 22.4 us -> 0 us
  between operations: 16.8 us -> 2.02 us
    unnamed x4 -> x0, waiting for transfers between devices: 340 us -> none
    pallas_call x0 -> x4, Pallas kernels: none -> 217 us  [the longest x1 104 us: gather_rows(): pl.pallas_call(gather_kernel, out_shape=jax.ShapeDtypeStruct((2, RING, RI...]
    all_gather x2 -> x0, waiting for transfers between devices: 206 us -> none  [the longest x1 104 us: local(): lax.all_gather(arrived_inputs, ('dp', 'sample'), axis=0, tiled=True)]
    dot_general x11 -> x8, matrix products: 139 us -> 77.1 us  [the longest x2 25.8 us: local(): rows = (back(grad_gate, w_gate) + back(grad_up, w_up)).astype(BF)]
    all_to_all x2 -> x0, blocking collectives: 23.6 us -> none  [the longest x1 12.8 us: local(): lax.all_to_all(sent_grads.reshape(layout), 'expert', split_axis=0, concat...]
    all_to_all x1 -> x0, starting transfers between devices: 22.1 us -> none  [local(): lax.all_to_all(row_sums, 'expert', split_axis=0, concat_axis=0, tiled=True)]
    psum x1 -> x0, blocking collectives: 9.09 us -> none  [local(): reward_total = lax.psum(own_reward, 'sample')]
  transfers between devices with their start and end apart: 4 -> 0, of which waited for: 3 -> 0; matrix products, arithmetic and copies ran while one was open for 13% -> 0% of each run, Pallas kernels for 0% -> 0%
where the time goes in v1:
time: 304 us; the launch traced here: 303 us
  Pallas kernels  217 us (71%)
  matrix products  77.1 us (25%)
  local copies, waits for them, and re-layouts  4.72 us (2%)
    pallas_call x1, Pallas kernels, gather_rows(): pl.pallas_call(gather_kernel, out_shape=jax.ShapeDtypeStruct((2, RING, RI...  104 us
    pallas_call x1, Pallas kernels, scatter_sum(): pl.pallas_call(scatter_kernel, out_shape=jax.ShapeDtypeStruct((ROWS // 2,...  57.7 us
    pallas_call x1, Pallas kernels, select_rows(): pl.pallas_call(select_kernel, grid=(blocks,), out_shape=(rows, rows, jax....  33.5 us
    dot_general x2, matrix products, local(): rows = (back(grad_gate, w_gate) + back(grad_up, w_up)).astype(BF)  25.8 us
    pallas_call x1, Pallas kernels, combine_rows(): pl.pallas_call(combine_kernel, grid=(blocks,), out_shape=jax.ShapeDtypeSt...  22 us
    dot_general x1, matrix products, local(): forward(g, w_down)  11.8 us
    dot_general x1, matrix products, local(): weigh(hidden, g).astype(BF)  11.6 us
    dot_general x1, matrix products, local(): forward(x, w_gate)  10.5 us

profile of v1, /device:TPU:1, one launch (start us, length us, event | category | flops | bytes accessed | tf_op | source)
XLA Modules:
  0.0 303.3 jit_solution(15967556251303084045)
XLA Ops:
  1.9 0.7 convert_convert_fusion
  2.6 0.8 fusion.9
  3.4 0.1 copy.45
  3.5 0.1 copy.42
  3.6 0.1 copy.40
  3.7 0.8 copy.44
  4.5 0.1 eq.15
  4.6 0.2 convert_reduce_fusion
  4.7 0.1 convert_element_type.55
  4.9 0.1 concatenate.10
  5.0 0.9 fusion.4
  5.9 0.9 pad_bitcast_fusion
  6.9 0.8 pad_maximum_fusion.own_ref
  7.7 103.6 %gather_rows.1 = bf16[2,4,4,4,40,4224]{5,4,3,2,1,0:T(8,128)(2,1)} custom-call(bf16[2,20,4224]{2,1,0:T(8,128)(2,1)} %pad_maximum_fusion.own_ref), custom_call_target="tpu_custom_call" | custom-call | tf_op jit(solution)/shard_map/gather_rows/pallas_call | solution.py:168
  111.3 33.5 %select_rows.1 = (bf16[2,768,4096]{2,1,0:T(8,128)(2,1)}, bf16[2,768,4096]{2,1,0:T(8,128)(2,1)}, bf16[16,160,128]{2,1,0:T(8,128)(2,1)}) custom-call(s32[1]{0:T(128)} %bitcast.group_ref, bf16[2,16,160,4224]{3,2,1,0:T(8,128)(2,1)} %bitcast.24), custom_call_target="tpu_custom_call" | custom-call | tf_op jit(solution)/shard_map/select_rows/pallas_call | solution.py:448
  144.8 0.0 copy-start
  144.8 10.5 %fusion.11 = f32[2,768,256]{2,1,0:T(8,128)} fusion(bf16[2,768,4096]{2,1,0:T(8,128)(2,1)} %get-tuple-element.9, bf16[2,256,4096]{2,1,0:T(8,128)(2,1)} %param.15), kind=kOutput, calls=%fused_computation.33 | convolution fusion | flops 3221225472 | bytes 18350080 | tf_op jit(solution)/shard_map/jcd,jfd->jcf/dot_general | solution.py:521
  155.3 0.0 copy-done
  155.3 6.8 %fusion.10 = f32[2,768,256]{2,1,0:T(8,128)} fusion(bf16[2,768,4096]{2,1,0:T(8,128)(2,1)S(1)} %copy-done, bf16[2,256,4096]{2,1,0:T(8,128)(2,1)} %param.16), kind=kOutput, calls=%fused_computation.32 | convolution fusion | flops 3221225472 | bytes 18350080 | tf_op jit(solution)/shard_map/jcd,jfd->jcf/dot_general | solution.py:521
  162.1 0.0 slice-start
  162.1 0.0 slice-start.1
  162.1 11.8 %multiply_convert_fusion.1 = (bf16[2,768,256]{2,1,0:T(8,128)(2,1)}, bf16[2,768,256]{2,1,0:T(8,128)(2,1)S(1)}) fusion(f32[2,768,256]{2,1,0:T(8,128)} %fusion.11, f32[2,768,256]{2,1,0:T(8,128)} %fusion.10, bf16[2,768,4096]{2,1,0:T(8,128)(2,1)} %get-tuple-element.8, bf16[2,256,4096]{2,1,0:T(8,128)(2,1)} %param.17), kind=kOutput, calls=%fused_computation.5 | convolution fusion | flops 3226337280 | bytes 21495808 | tf_op jit(solution)/shard_map/jcd,jfd->jcf/dot_general | solution.py:521
  173.9 0.0 slice-start.2
  173.9 0.0 copy-start.1
  173.9 11.6 %convolution_convert_fusion = bf16[2,256,4096]{2,1,0:T(8,128)(2,1)} fusion(bf16[2,768,4096]{2,1,0:T(8,128)(2,1)} %get-tuple-element.8, f32[2,768,256]{2,1,0:T(8,128)} %fusion.10, f32[2,768,256]{2,1,0:T(8,128)} %fusion.11), kind=kOutput, calls=%fused_computation.1 | convolution fusion | flops 3225681920 | bytes 19922944 | tf_op jit(solution)/shard_map/jcf,jcd->jfd/dot_general | solution.py:534
  185.5 0.0 slice-done
  185.5 0.0 slice-done.1
  185.5 0.0 slice-done.2
  185.5 0.0 copy-done.1
  185.5 5.4 %convolution_convert_fusion.1 = bf16[2,256,4096]{2,1,0:T(8,128)(2,1)} fusion(bf16[2,768,256]{2,1,0:T(8,128)(2,1)S(1)} %copy-done.1, bf16[2,768,4096]{2,1,0:T(8,128)(2,1)S(1)} %bitcast.27), kind=kOutput, calls=%fused_computation.2 | convolution fusion | flops 3223322624 | bytes 17563648 | tf_op jit(solution)/shard_map/jcf,jcd->jfd/dot_general | solution.py:533
  190.9 0.0 copy-start.3
  190.9 5.4 %convolution_convert_fusion.2 = bf16[2,256,4096]{2,1,0:T(8,128)(2,1)} fusion(bf16[2,768,256]{2,1,0:T(8,128)(2,1)S(1)} %get-tuple-element.11, bf16[2,768,4096]{2,1,0:T(8,128)(2,1)S(1)} %bitcast.27), kind=kOutput, calls=%fused_computation.3 | convolution fusion | flops 3223322624 | bytes 17563648 | tf_op jit(solution)/shard_map/jcf,jcd->jfd/dot_general | solution.py:532
  196.3 0.0 copy-done.3
  196.3 0.0 copy-start.2
  196.3 10.0 %fusion.12 = f32[2,768,4096]{2,1,0:T(8,128)} fusion(bf16[2,768,256]{2,1,0:T(8,128)(2,1)S(1)} %get-tuple-element.11, bf16[2,256,4096]{2,1,0:T(8,128)(2,1)S(1)} %copy-done.3), kind=kOutput, calls=%fused_computation.34 | convolution fusion | flops 3221225472 | bytes 30146560 | tf_op jit(solution)/shard_map/jcf,jfd->jcd/dot_general | solution.py:527
  206.3 0.0 copy-done.2
  206.3 15.7 %add_convert_fusion.r_ref = bf16[2,768,4096]{2,1,0:T(8,128)(2,1)} fusion(f32[2,768,4096]{2,1,0:T(8,128)} %fusion.12, bf16[2,768,256]{2,1,0:T(8,128)(2,1)S(1)} %copy-done.2, bf16[2,256,4096]{2,1,0:T(8,128)(2,1)} %param.16), kind=kOutput, calls=%fused_computation | convolution fusion | flops 3233808384 | bytes 42729472 | tf_op jit(solution)/shard_map/jcf,jfd->jcd/dot_general | solution.py:527
  222.0 22.0 %combine_rows.1 = bf16[16,160,4096]{2,1,0:T(8,128)(2,1)} custom-call(bf16[16,160,128]{2,1,0:T(8,128)(2,1)} %get-tuple-element.7.pick_ref, bf16[2,768,4096]{2,1,0:T(8,128)(2,1)} %add_convert_fusion.r_ref), custom_call_target="tpu_custom_call" | custom-call | tf_op jit(solution)/shard_map/combine_rows/pallas_call | solution.py:475
  244.0 57.7 %scatter_sum.1 = bf16[20,4096]{1,0:T(8,128)(2,1)} custom-call(bf16[4,4,4,40,4096]{4,3,2,1,0:T(8,128)(2,1)} %bitcast.25), custom_call_target="tpu_custom_call" | custom-call | tf_op jit(solution)/shard_map/scatter_sum/pallas_call | solution.py:376
  301.7 1.6 copy.55
  (5 shorter events, 0.0 us)
Async XLA Ops:
  144.8 10.5 %copy-start = (bf16[2,768,4096]{2,1,0:T(8,128)(2,1)S(1)}, bf16[2,768,4096]{2,1,0:T(8,128)(2,1)}, u32[]{:S(2)}) copy-start(bf16[2,768,4096]{2,1,0:T(8,128)(2,1)} %get-tuple-element.9) | copy-start | bytes 37748740
  162.1 23.4 %slice-start = ((s8[12582912]{0:T(1024)(128)(4,1)}), s8[4194304]{0:T(1024)(128)(4,1)S(1)}, s32[]{:S(2)}) async-start(s8[12582912]{0:T(1024)(128)(4,1)} %bitcast.26), calls=%async_computation | async-start | bytes 8388608
  162.1 23.4 %slice-start.1 = ((s8[12582912]{0:T(1024)(128)(4,1)}), s8[4194304]{0:T(1024)(128)(4,1)S(1)}, s32[]{:S(2)}) async-start(s8[12582912]{0:T(1024)(128)(4,1)} %bitcast.26), calls=%async_computation.1 | async-start | bytes 8388608
  173.9 11.6 %slice-start.2 = ((s8[12582912]{0:T(1024)(128)(4,1)}), s8[4194304]{0:T(1024)(128)(4,1)S(1)}, s32[]{:S(2)}) async-start(s8[12582912]{0:T(1024)(128)(4,1)} %bitcast.26), calls=%async_computation.2 | async-start | bytes 8388608
  173.9 11.6 %copy-start.1 = (bf16[2,768,256]{2,1,0:T(8,128)(2,1)S(1)}, bf16[2,768,256]{2,1,0:T(8,128)(2,1)}, u32[]{:S(2)}) copy-start(bf16[2,768,256]{2,1,0:T(8,128)(2,1)} %get-tuple-element.10) | copy-start | bytes 2359300
  190.9 5.4 %copy-start.3 = (bf16[2,256,4096]{2,1,0:T(8,128)(2,1)S(1)}, bf16[2,256,4096]{2,1,0:T(8,128)(2,1)}, u32[]{:S(2)}) copy-start(bf16[2,256,4096]{2,1,0:T(8,128)(2,1)} %param.15) | copy-start | bytes 12582916
  196.3 10.0 %copy-start.2 = (bf16[2,768,256]{2,1,0:T(8,128)(2,1)S(1)}, bf16[2,768,256]{2,1,0:T(8,128)(2,1)}, u32[]{:S(2)}) copy-start(bf16[2,768,256]{2,1,0:T(8,128)(2,1)} %get-tuple-element.10) | copy-start | bytes 2359300

commit v2 on v1

--- a/solution.py
+++ b/solution.py
@@ -182,19 +182,25 @@
     )(own)
 
 
+GROUP = 160
+SLOTS = 48
+
 HALF = WIDTH // 2
-WIDTHS = (768, 640, 640)
-STARTS = (0, 768, 1408)
+WIDTHS = (384, 384, 256, 384, 256, 384)
+STARTS = (0, 384, 768, 1024, 1408, 1664)
+WIDEST = 384
+STREAMS = 6
+STREAM_COPIES = 22
 AHEAD = (3, 1)
 BEHIND = (2, 0)
 
 
-def scatter_kernel(p_ref, out_ref, *scratch):
-    acc, mate, fa, ma, pa, fb, mb, pb, fc, mc, pc = [scratch[3 * i : 3 * i + 3] for i in range(11)]
-    done, other_done, load, load_far, far_in, send, recv = scratch[33:]
+def finish_kernel(gg_ref, gu_ref, pick_ref, wg_ref, wu_ref, out_ref, *scratch):
+    n = STREAMS
+    acc, mate, fa, ma, pa, fb, mb, pb, fc, mc, pc = [scratch[n * i : n * i + n] for i in range(11)]
+    give, weights, rows, done, other_done, wsem, send, recv = scratch[11 * n :]
     at, core = place()
     partner = device(at, 1 - core)
-    greet(at, core)
     copies = {}
     every = pl.ds(0, RING)
     offset = (0, -1, 1, 2)
@@ -209,35 +215,72 @@
         to = {**at, **over}
         return to["z"], to["y"], to["x"]
 
-    def plane_at(p, by):
-        d1, d2, d3 = ORDERS[p]
-        return spot(**{d1: every, d2: every, d3: coord(d3, by)})
-
-    def columns(p, side):
-        return pl.ds(pl.multiple_of(side * HALF + STARTS[p], 128), WIDTHS[p])
-
-    def push(p, key, k, src, dst, peer):
-        copy = remote(src, dst, send.at[p, k], recv.at[p, k], peer)
+    def order(s):
+        return ORDERS[s % 3]
+
+    def push(s, key, k, src, dst, peer):
+        copy = remote(src, dst, send.at[s, k], recv.at[s, k], peer)
         copy.start()
-        copies[(p,) + key] = copy
-
-    loads = {}
-    for n, by in enumerate((2, 1, -1, 0)):
-        for p in range(3):
-            where = plane_at(p, by)
-            far = remote(
-                p_ref.at[where + (slice(None), columns(p, 1 - core))],
-                mate[p].at[where],
-                load_far.at[p, n],
-                far_in.at[p, n],
-                partner,
+        copies[(s,) + key] = copy
+
+    turns = [(s, far) for c in (0, 3) for far in (True, False) for s in range(c, c + 3)]
+
+    def fetch(turn):
+        s, far = turns[turn]
+        side = 1 - core if far else core
+        columns = pl.ds(pl.multiple_of(side * HALF + STARTS[s], 128), WIDTHS[s])
+        got = []
+        for k, ref in enumerate((wg_ref, wu_ref)):
+            to = weights.at[turn % 2, k, :, :, pl.ds(0, WIDTHS[s])]
+            got.append(pltpu.make_async_copy(ref.at[:, :, columns], to, wsem.at[turn % 2, k]))
+            got[-1].start()
+        return got
+
+    fetched = {0: fetch(0)}
+
+    def compute(turn):
+        s, far = turns[turn]
+        w = WIDTHS[s]
+        slot = turn % 2
+        if turn + 1 < len(turns):
+            fetched[turn + 1] = fetch(turn + 1)
+        for copy in fetched[turn]:
+            copy.wait()
+        part = 8 * SLOTS
+
+        def product(i, carry):
+            j, half = i // 2, i % 2
+            take = pl.ds(pl.multiple_of(half * part, part), part)
+            total = jnp.dot(gg_ref[j, take, :], weights[slot, 0, j, :, :w], preferred_element_type=F32)
+            total += jnp.dot(gu_ref[j, take, :], weights[slot, 1, j, :, :w], preferred_element_type=F32)
+            total = total.astype(BF)
+            for l in range(8):
+                rows[half * 8 + l, j, :, :w] = total[l * SLOTS : (l + 1) * SLOTS]
+            return carry
+
+        lax.fori_loop(0, 4, product, 0)
+        if far:
+            if s >= 3:
+                copies[s - 3, "far"].wait_send()
+        else:
+            copies[s, "far"].wait_recv()
+
+        def place_rows(l, carry):
+            z, y = l // RING, l % RING
+            total = jnp.dot(
+                pick_ref[l, :, : 2 * SLOTS], rows[l, :, :, :w].reshape(2 * SLOTS, w), preferred_element_type=F32
             )
-            far.start()
-            own = pltpu.make_async_copy(
-                p_ref.at[where + (slice(None), columns(p, core))], acc[p].at[where], load.at[p, n]
-            )
-            own.start()
-            loads[p, by] = (own, far)
+            for x in range(RING):
+                piece = total[x * ROWS : (x + 1) * ROWS]
+                if far:
+                    give[s % 3, z, y, x, :, :w] = piece.astype(BF)
+                else:
+                    acc[s][z, y, x] = (piece + mate[s][z, y, x].astype(F32)).astype(BF)
+            return carry
+
+        lax.fori_loop(0, RING * RING, place_rows, 0)
+        if far:
+            push(s, ("far",), 21, give.at[s % 3, :, :, :, :, pl.ds(0, w)], mate[s], partner)
 
     def add(dst, index, *terms):
         total = dst[index].astype(F32)
@@ -245,109 +288,122 @@
             total = total + ref[where].astype(F32)
         dst[index] = total.astype(BF)
 
-    def ready(p, by):
-        own, far = loads[p, by]
-        own.wait()
-        far.wait_recv()
-        d1, d2, d3 = ORDERS[p]
-
-        def body(i, carry):
-            where = spot(**{d1: i % RING, d2: i // RING, d3: coord(d3, by)})
-            add(acc[p], where, (mate[p], where))
-            return carry
-
-        lax.fori_loop(0, RING * RING, body, 0)
-
-    def line(p, r, by):
-        d1, d2, d3 = ORDERS[p]
-        return acc[p].at[spot(**{d1: every, d2: coord(d2, offset[r]), d3: coord(d3, by)})]
-
-    def add_line(p, r, by, *terms, first=0, count=RING):
-        d1, d2, d3 = ORDERS[p]
+    def line(s, r, by):
+        d1, d2, d3 = order(s)
+        return acc[s].at[spot(**{d1: every, d2: coord(d2, offset[r]), d3: coord(d3, by)})]
+
+    def add_line(s, r, by, *terms, first=0, count=RING):
+        d1, d2, d3 = order(s)
 
         def body(i, carry):
             where = spot(**{d1: i, d2: coord(d2, offset[r]), d3: coord(d3, by)})
-            add(acc[p], where, *[(ref, (r, i) if lead else (i,)) for ref, lead in terms])
+            add(acc[s], where, *[(ref, (r, i) if lead else (i,)) for ref, lead in terms])
             return carry
 
         lax.fori_loop(first, first + count, body, 0)
 
-    for p in range(3):
-        ready(p, 2)
-        for r in (3, 2, 1, 0):
-            push(p, ("fa", r), r, line(p, r, 2), fa[p].at[r], near(ORDERS[p][2], 1 if r in AHEAD else -1))
-    for p in range(3):
-        ready(p, 1)
-        for r in BEHIND:
-            push(p, ("ma", r), 4 + r, line(p, r, 1), ma[p].at[r], near(ORDERS[p][2], 1))
-    for p in range(3):
-        ready(p, -1)
-        for r in AHEAD:
-            push(p, ("pa", r), 8 + r, line(p, r, -1), pa[p].at[r], near(ORDERS[p][2], -1))
-    for p in range(3):
-        ready(p, 0)
-    for r in (3, 2, 1, 0):
-        for p in range(3):
-            copies[p, "fa", r].wait_recv()
-            if r in AHEAD:
-                add_line(p, r, 1, (fa[p], True))
-                push(p, ("ma", r), 4 + r, line(p, r, 1), ma[p].at[r], near(ORDERS[p][2], 1))
-            else:
-                add_line(p, r, -1, (fa[p], True))
-                push(p, ("pa", r), 8 + r, line(p, r, -1), pa[p].at[r], near(ORDERS[p][2], -1))
-
-    def piece(p, r, half):
-        d1, d2, d3 = ORDERS[p]
-        return acc[p].at[spot(**{d1: pl.ds(2 * half, 2), d2: coord(d2, offset[r])})]
+    def piece(s, r, half):
+        d1, d2, d3 = order(s)
+        return acc[s].at[spot(**{d1: pl.ds(2 * half, 2), d2: coord(d2, offset[r])})]
 
     def half_of(ref, half):
         return ref.at[pl.ds(2 * half, 2)]
 
-    for r in (3, 2, 1, 0):
-        for p in range(3):
-            copies[p, "ma", r].wait_recv()
-            copies[p, "pa", r].wait_recv()
-            add_line(p, r, 0, (ma[p], True), (pa[p], True))
-            d2 = ORDERS[p][1]
-            if r == 3:
-                push(p, ("fb", 0), 12, piece(p, 3, 0), half_of(fb[p], 0), near(d2, 1))
-                push(p, ("fb", 1), 13, piece(p, 3, 1), half_of(fb[p], 1), near(d2, -1))
-            if r == 2:
-                push(p, ("mb", 1), 15, piece(p, 2, 1), half_of(mb[p], 1), near(d2, 1))
-            if r == 1:
-                push(p, ("pb", 0), 16, piece(p, 1, 0), half_of(pb[p], 0), near(d2, -1))
-    for p in range(3):
-        d2 = ORDERS[p][1]
-        copies[p, "fb", 0].wait_recv()
-        add_line(p, 2, 0, (fb[p], False), first=0, count=2)
-        push(p, ("mb", 0), 14, piece(p, 2, 0), half_of(mb[p], 0), near(d2, 1))
-        copies[p, "fb", 1].wait_recv()
-        add_line(p, 1, 0, (fb[p], False), first=2, count=2)
-        push(p, ("pb", 1), 17, piece(p, 1, 1), half_of(pb[p], 1), near(d2, -1))
-
-    def cell(p, by):
-        d1 = ORDERS[p][0]
+    def cell(s, by):
+        d1 = order(s)[0]
         return spot(**{d1: coord(d1, by)})
 
-    for p in range(3):
-        d1 = ORDERS[p][0]
-        for half in (0, 1):
-            copies[p, "mb", half].wait_recv()
-            copies[p, "pb", half].wait_recv()
-        add_line(p, 0, 0, (mb[p], False), (pb[p], False))
-        push(p, ("fc",), 18, acc[p].at[cell(p, 2)], fc[p], near(d1, 1))
-        push(p, ("pc",), 20, acc[p].at[cell(p, -1)], pc[p], near(d1, -1))
-    for p in range(3):
-        d1 = ORDERS[p][0]
-        copies[p, "fc"].wait_recv()
-        add(acc[p], cell(p, 1), (fc[p], ...))
-        push(p, ("mc",), 19, acc[p].at[cell(p, 1)], mc[p], near(d1, 1))
-    for p in range(3):
-        copies[p, "pc"].wait_recv()
-        copies[p, "mc"].wait_recv()
-        own = acc[p][cell(p, 0)].astype(F32) + pc[p][...].astype(F32) + mc[p][...].astype(F32)
-        done[:, STARTS[p] : STARTS[p] + WIDTHS[p]] = own.astype(BF)
-    last = remote(done, other_done, send.at[3, 0], recv.at[3, 0], partner)
+    def travel(streams):
+        for s in streams:
+            d3 = order(s)[2]
+            for r in (3, 2, 1, 0):
+                push(s, ("fa", r), r, line(s, r, 2), fa[s].at[r], near(d3, 1 if r in AHEAD else -1))
+            for r in BEHIND:
+                push(s, ("ma", r), 4 + r, line(s, r, 1), ma[s].at[r], near(d3, 1))
+            for r in AHEAD:
+                push(s, ("pa", r), 8 + r, line(s, r, -1), pa[s].at[r], near(d3, -1))
+        yield
+        for r in (3, 2, 1, 0):
+            for s in streams:
+                d3 = order(s)[2]
+                copies[s, "fa", r].wait_recv()
+                if r in AHEAD:
+                    add_line(s, r, 1, (fa[s], True))
+                    push(s, ("ma", r), 4 + r, line(s, r, 1), ma[s].at[r], near(d3, 1))
+                else:
+                    add_line(s, r, -1, (fa[s], True))
+                    push(s, ("pa", r), 8 + r, line(s, r, -1), pa[s].at[r], near(d3, -1))
+                yield
+        for r in (3, 2, 1, 0):
+            for s in streams:
+                d2 = order(s)[1]
+                copies[s, "ma", r].wait_recv()
+                copies[s, "pa", r].wait_recv()
+                add_line(s, r, 0, (ma[s], True), (pa[s], True))
+                if r == 3:
+                    push(s, ("fb", 0), 12, piece(s, 3, 0), half_of(fb[s], 0), near(d2, 1))
+                    push(s, ("fb", 1), 13, piece(s, 3, 1), half_of(fb[s], 1), near(d2, -1))
+                if r == 2:
+                    push(s, ("mb", 1), 15, piece(s, 2, 1), half_of(mb[s], 1), near(d2, 1))
+                if r == 1:
+                    push(s, ("pb", 0), 16, piece(s, 1, 0), half_of(pb[s], 0), near(d2, -1))
+                yield
+        for s in streams:
+            d2 = order(s)[1]
+            copies[s, "fb", 0].wait_recv()
+            add_line(s, 2, 0, (fb[s], False), first=0, count=2)
+            push(s, ("mb", 0), 14, piece(s, 2, 0), half_of(mb[s], 0), near(d2, 1))
+            copies[s, "fb", 1].wait_recv()
+            add_line(s, 1, 0, (fb[s], False), first=2, count=2)
+            push(s, ("pb", 1), 17, piece(s, 1, 1), half_of(pb[s], 1), near(d2, -1))
+            yield
+        for s in streams:
+            d1 = order(s)[0]
+            for half in (0, 1):
+                copies[s, "mb", half].wait_recv()
+                copies[s, "pb", half].wait_recv()
+            add_line(s, 0, 0, (mb[s], False), (pb[s], False))
+            push(s, ("fc",), 18, acc[s].at[cell(s, 2)], fc[s], near(d1, 1))
+            push(s, ("pc",), 20, acc[s].at[cell(s, -1)], pc[s], near(d1, -1))
+            yield
+        for s in streams:
+            d1 = order(s)[0]
+            copies[s, "fc"].wait_recv()
+            add(acc[s], cell(s, 1), (fc[s], ...))
+            push(s, ("mc",), 19, acc[s].at[cell(s, 1)], mc[s], near(d1, 1))
+            yield
+        for s in streams:
+            copies[s, "pc"].wait_recv()
+            copies[s, "mc"].wait_recv()
+            own = acc[s][cell(s, 0)].astype(F32) + pc[s][...].astype(F32) + mc[s][...].astype(F32)
+            done[:, STARTS[s] : STARTS[s] + WIDTHS[s]] = own.astype(BF)
+            yield
+
+    def forward(journey, count):
+        for _ in range(count):
+            next(journey, None)
+
+    greet(at, core)
+    for turn in range(6):
+        compute(turn)
+    early = travel((0, 1, 2))
+    forward(early, 1)
+    for turn in (6, 7, 8):
+        compute(turn)
+    forward(early, 3)
+    for turn in (9, 10):
+        compute(turn)
+    forward(early, 3)
+    compute(11)
+    late = travel((3, 4, 5))
+    forward(late, 1)
+    forward(early, 9)
+    for _ in range(12):
+        forward(early, 1)
+        forward(late, 1)
+    forward(early, 60)
+    forward(late, 60)
+    last = remote(done, other_done, send.at[n, 0], recv.at[n, 0], partner)
     last.start()
     last.wait_recv()
 
@@ -362,38 +418,41 @@
         out_ref[:, HALF:] = done[20:40]
 
     last.wait_send()
-    for copy in copies.values():
-        copy.wait_send()
-    for _, far in loads.values():
-        far.wait_send()
-
-
-def scatter_sum(partial):
+    for key, copy in copies.items():
+        if key[1] != "far" or key[0] >= 3:
+            copy.wait_send()
+
+
+def finish(grad_gate, grad_up, pick, w_gate, w_up):
     full = [pltpu.VMEM((RING, RING, RING, ROWS, w), BF) for w in WIDTHS]
     lines = [pltpu.VMEM((RING, RING, ROWS, w), BF) for w in WIDTHS]
     line = [pltpu.VMEM((RING, ROWS, w), BF) for w in WIDTHS]
     cell = [pltpu.VMEM((ROWS, w), BF) for w in WIDTHS]
+    hidden = w_gate.shape[1]
     return pl.pallas_call(
-        scatter_kernel,
+        finish_kernel,
         out_shape=jax.ShapeDtypeStruct((ROWS // 2, WIDTH), BF),
-        in_specs=[pl.BlockSpec(memory_space=pl.ANY)],
+        in_specs=[pl.BlockSpec(memory_space=pltpu.VMEM)] * 3 + [pl.BlockSpec(memory_space=pl.ANY)] * 2,
         out_specs=pl.BlockSpec(memory_space=pltpu.VMEM),
         scratch_shapes=full * 2
         + lines * 3
         + line * 3
         + cell * 3
-        + [pltpu.VMEM((ROWS, HALF), BF)] * 2
-        + [pltpu.SemaphoreType.DMA((3, 4))] * 3
-        + [pltpu.SemaphoreType.DMA((4, 21))] * 2,
+        + [
+            pltpu.VMEM((3, RING, RING, RING, ROWS, WIDEST), BF),
+            pltpu.VMEM((2, 2, 2, hidden, WIDEST), BF),
+            pltpu.VMEM((RING * RING, 2, SLOTS, WIDEST), BF),
+            pltpu.VMEM((ROWS, HALF), BF),
+            pltpu.VMEM((ROWS, HALF), BF),
+            pltpu.SemaphoreType.DMA((2, 2)),
+            pltpu.SemaphoreType.DMA((STREAMS + 1, STREAM_COPIES)),
+            pltpu.SemaphoreType.DMA((STREAMS + 1, STREAM_COPIES)),
+        ],
         compiler_params=pltpu.CompilerParams(
             collective_id=1, has_side_effects=True, vmem_limit_bytes=60 * 1024 * 1024
         ),
-        name="scatter_sum",
-    )(partial)
-
-
-GROUP = 160
-SLOTS = 48
+        name="finish",
+    )(grad_gate, grad_up, pick, w_gate, w_up)
 
 
 def turned(a, b):
@@ -462,29 +521,6 @@
     )(group, everything)
 
 
-def combine_kernel(pick_ref, r_ref, out_ref):
-    for start in range(0, WIDTH, 1024):
-        cols = slice(start, start + 1024)
-        total = jnp.dot(pick_ref[0, :, :SLOTS], r_ref[0, :, cols], preferred_element_type=F32)
-        total += jnp.dot(pick_ref[0, :, SLOTS : 2 * SLOTS], r_ref[1, :, cols], preferred_element_type=F32)
-        out_ref[0, :, cols] = total.astype(BF)
-
-
-def combine_rows(pick, rows):
-    blocks = pick.shape[0]
-    return pl.pallas_call(
-        combine_kernel,
-        grid=(blocks,),
-        out_shape=jax.ShapeDtypeStruct((blocks, GROUP, WIDTH), BF),
-        in_specs=[
-            pl.BlockSpec((1, GROUP, 128), lambda b: (b, 0, 0)),
-            pl.BlockSpec((2, SLOTS, WIDTH), lambda b: (0, b, 0)),
-        ],
-        out_specs=pl.BlockSpec((1, GROUP, WIDTH), lambda b: (b, 0, 0)),
-        name="combine_rows",
-    )(pick, rows)
-
-
 def three(values):
     high = lax.reduce_precision(values, 8, 7)
     middle = lax.reduce_precision(values - high, 8, 7)
@@ -516,7 +552,6 @@
     group = lax.axis_index("expert").astype(jnp.int32).reshape(1)
     x, g, pick = select_rows(group, everything)
     forward = functools.partial(jnp.einsum, "jcd,jfd->jcf", preferred_element_type=F32)
-    back = functools.partial(jnp.einsum, "jcf,jfd->jcd", preferred_element_type=F32)
     weigh = functools.partial(jnp.einsum, "jcf,jcd->jfd", preferred_element_type=F32)
     pre_gate, pre_up, grad_hidden = forward(x, w_gate), forward(x, w_up), forward(g, w_down)
     prob = jax.nn.sigmoid(pre_gate)
@@ -524,9 +559,7 @@
     hidden = (active * pre_up).astype(BF)
     grad_gate = (grad_hidden * pre_up * (prob * (1.0 + pre_gate * (1.0 - prob)))).astype(BF)
     grad_up = (grad_hidden * active).astype(BF)
-    rows = (back(grad_gate, w_gate) + back(grad_up, w_up)).astype(BF)
-    partial = combine_rows(pick, rows).reshape(RING, RING, RING, ROWS, WIDTH)
-    grad_tokens = scatter_sum(partial)
+    grad_tokens = finish(grad_gate, grad_up, pick, w_gate, w_up)
     return (
         grad_tokens,
         weigh(grad_gate, x).astype(BF),

time: 304 us -> 308 us (1.013)
  Pallas kernels: 217 us -> 242 us
  matrix products: 77.1 us -> 55.3 us
    dot_general x2 -> x0, matrix products: 25.8 us -> none  [local(): rows = (back(grad_gate, w_gate) + back(grad_up, w_up)).astype(BF)]
    pallas_call x2 -> x1, Pallas kernels: 79.7 us -> 105 us  [finish(): pl.pallas_call(finish_kernel, out_shape=jax.ShapeDtypeStruct((ROWS // 2,...]
    dot_general x1, matrix products: 5.39 us -> 9.74 us  [local(): weigh(grad_up, x).astype(BF)]
    dot_general x1, matrix products: 5.36 us -> 9.69 us  [local(): weigh(grad_gate, x).astype(BF)]
where the time goes in v2:
time: 308 us
  Pallas kernels  242 us (79%)
  matrix products  55.3 us (18%)
  local copies, waits for them, and re-layouts  5.3 us (2%)
    pallas_call x1, Pallas kernels, finish(): pl.pallas_call(finish_kernel, out_shape=jax.ShapeDtypeStruct((ROWS // 2,...  105 us
    pallas_call x1, Pallas kernels, gather_rows(): pl.pallas_call(gather_kernel, out_shape=jax.ShapeDtypeStruct((2, RING, RI...  104 us
    pallas_call x1, Pallas kernels, select_rows(): pl.pallas_call(select_kernel, grid=(blocks,), out_shape=(rows, rows, jax....  33.7 us
    dot_general x1, matrix products, local(): forward(g, w_down)  11.5 us
    dot_general x1, matrix products, local(): weigh(hidden, g).astype(BF)  9.75 us
    dot_general x1, matrix products, local(): weigh(grad_up, x).astype(BF)  9.74 us
    dot_general x1, matrix products, local(): weigh(grad_gate, x).astype(BF)  9.69 us
    dot_general x1, matrix products, local(): forward(x, w_gate)  7.83 us

profile of v2, /device:TPU:1, one launch (start us, length us, event | category | flops | bytes accessed | tf_op | source)
XLA Modules:
  0.0 307.7 jit_solution(8248270643706679871)
XLA Ops:
  1.9 0.7 convert_convert_fusion
  2.6 0.8 fusion.9
  3.4 0.1 copy.45
  3.5 0.1 copy.42
  3.6 0.1 copy.40
  3.7 0.8 copy.44
  4.5 0.1 eq.15
  4.6 0.2 convert_reduce_fusion
  4.7 0.1 convert_element_type.52
  4.9 0.1 concatenate.10
  5.0 0.9 fusion.4
  5.9 0.9 pad_bitcast_fusion
  6.9 0.8 pad_maximum_fusion.own_ref
  7.7 103.6 %gather_rows.1 = bf16[2,4,4,4,40,4224]{5,4,3,2,1,0:T(8,128)(2,1)} custom-call(bf16[2,20,4224]{2,1,0:T(8,128)(2,1)} %pad_maximum_fusion.own_ref), custom_call_target="tpu_custom_call" | custom-call | tf_op jit(solution)/shard_map/gather_rows/pallas_call | solution.py:168
  111.3 33.7 %select_rows.1 = (bf16[2,768,4096]{2,1,0:T(8,128)(2,1)}, bf16[2,768,4096]{2,1,0:T(8,128)(2,1)}, bf16[16,160,128]{2,1,0:T(8,128)(2,1)}) custom-call(s32[1]{0:T(128)} %bitcast.group_ref, bf16[2,16,160,4224]{3,2,1,0:T(8,128)(2,1)} %bitcast.19), custom_call_target="tpu_custom_call" | custom-call | tf_op jit(solution)/shard_map/select_rows/pallas_call | solution.py:507
  145.0 0.0 copy-start
  145.0 7.8 %fusion.11 = f32[2,768,256]{2,1,0:T(8,128)S(1)} fusion(bf16[2,768,4096]{2,1,0:T(8,128)(2,1)} %get-tuple-element.8, bf16[2,256,4096]{2,1,0:T(8,128)(2,1)} %wg_ref.1), kind=kOutput, calls=%fused_computation.32 | convolution fusion | flops 3221225472 | bytes 18350080 | tf_op jit(solution)/shard_map/jcd,jfd->jcf/dot_general | solution.py:556
  152.8 1.5 copy-done
  154.4 6.8 %fusion.10 = f32[2,768,256]{2,1,0:T(8,128)} fusion(bf16[2,768,4096]{2,1,0:T(8,128)(2,1)S(1)} %copy-done, bf16[2,256,4096]{2,1,0:T(8,128)(2,1)} %wu_ref.1), kind=kOutput, calls=%fused_computation.31 | convolution fusion | flops 3221225472 | bytes 18350080 | tf_op jit(solution)/shard_map/jcd,jfd->jcf/dot_general | solution.py:556
  161.1 0.0 copy-start.4
  161.1 11.5 %multiply_convert_fusion.1 = (bf16[2,768,256]{2,1,0:T(8,128)(2,1)}, bf16[2,768,256]{2,1,0:T(8,128)(2,1)}) fusion(f32[2,768,256]{2,1,0:T(8,128)S(1)} %fusion.11, f32[2,768,256]{2,1,0:T(8,128)} %fusion.10, bf16[2,768,4096]{2,1,0:T(8,128)(2,1)} %get-tuple-element.7, bf16[2,256,4096]{2,1,0:T(8,128)(2,1)} %param.17), kind=kOutput, calls=%fused_computation.4 | convolution fusion | flops 3226337280 | bytes 21495808 | tf_op jit(solution)/shard_map/jcd,jfd->jcf/dot_general | solution.py:556
  172.6 0.0 copy-done.4
  172.6 9.8 %convolution_convert_fusion = bf16[2,256,4096]{2,1,0:T(8,128)(2,1)} fusion(bf16[2,768,4096]{2,1,0:T(8,128)(2,1)} %get-tuple-element.7, f32[2,768,256]{2,1,0:T(8,128)S(1)} %copy-done.4, f32[2,768,256]{2,1,0:T(8,128)S(1)} %fusion.11), kind=kOutput, calls=%fused_computation | convolution fusion | flops 3225681920 | bytes 19922944 | tf_op jit(solution)/shard_map/jcf,jcd->jfd/dot_general | solution.py:567
  182.4 0.0 copy-start.2
  182.4 105.2 %finish.1 = bf16[20,4096]{1,0:T(8,128)(2,1)} custom-call(bf16[2,768,256]{2,1,0:T(8,128)(2,1)} %get-tuple-element.11.gg_ref, bf16[2,768,256]{2,1,0:T(8,128)(2,1)} %get-tuple-element.10.gu_ref, bf16[16,160,128]{2,1,0:T(8,128)(2,1)} %get-tuple-element.9.pick_ref, bf16[2,256,4096]{2,1,0:T(8,128)(2,1)} %wg_ref.1, bf16[2,256,4096]{2,1,0:T(8,128)(2,1)} %wu_ref.1), custom_call_target="tpu_custom_call" | custom-call | tf_op jit(solution)/shard_map/finish/pallas_call | solution.py:432
  287.6 0.0 copy-done.2
  287.6 0.0 copy-start.1
  287.6 9.7 %convolution_convert_fusion.1 = bf16[2,256,4096]{2,1,0:T(8,128)(2,1)} fusion(bf16[2,768,256]{2,1,0:T(8,128)(2,1)S(1)} %copy-done.2, bf16[2,768,4096]{2,1,0:T(8,128)(2,1)} %get-tuple-element.8), kind=kOutput, calls=%fused_computation.1 | convolution fusion | flops 3223322624 | bytes 17563648 | tf_op jit(solution)/shard_map/jcf,jcd->jfd/dot_general | solution.py:566
  297.4 0.0 copy-done.1
  297.4 0.0 copy-start.3
  297.4 9.7 %convolution_convert_fusion.2 = bf16[2,256,4096]{2,1,0:T(8,128)(2,1)} fusion(bf16[2,768,256]{2,1,0:T(8,128)(2,1)S(1)} %copy-done.1, bf16[2,768,4096]{2,1,0:T(8,128)(2,1)} %get-tuple-element.8), kind=kOutput, calls=%fused_computation.2 | convolution fusion | flops 3223322624 | bytes 17563648 | tf_op jit(solution)/shard_map/jcf,jcd->jfd/dot_general | solution.py:565
  307.1 0.0 copy-done.3
  307.1 0.7 copy.55
  (4 shorter events, 0.0 us)
Async XLA Ops:
  145.0 9.4 %copy-start = (bf16[2,768,4096]{2,1,0:T(8,128)(2,1)S(1)}, bf16[2,768,4096]{2,1,0:T(8,128)(2,1)}, u32[]{:S(2)}) copy-start(bf16[2,768,4096]{2,1,0:T(8,128)(2,1)} %get-tuple-element.8) | copy-start | bytes 37748740
  161.1 11.5 %copy-start.4 = (f32[2,768,256]{2,1,0:T(8,128)S(1)}, f32[2,768,256]{2,1,0:T(8,128)}, u32[]{:S(2)}) copy-start(f32[2,768,256]{2,1,0:T(8,128)} %fusion.10) | copy-start | bytes 4718596
  182.4 105.2 %copy-start.2 = (bf16[2,768,256]{2,1,0:T(8,128)(2,1)S(1)}, bf16[2,768,256]{2,1,0:T(8,128)(2,1)}, u32[]{:S(2)}) copy-start(bf16[2,768,256]{2,1,0:T(8,128)(2,1)} %get-tuple-element.10.gu_ref) | copy-start | bytes 2359300
  287.6 9.8 %copy-start.1 = (bf16[2,768,256]{2,1,0:T(8,128)(2,1)S(1)}, bf16[2,768,256]{2,1,0:T(8,128)(2,1)}, u32[]{:S(2)}) copy-start(bf16[2,768,256]{2,1,0:T(8,128)(2,1)} %get-tuple-element.11.gg_ref) | copy-start | bytes 2359300
  297.4 9.7 %copy-start.3 = (bf16[20,4096]{1,0:T(8,128)(2,1)S(1)}, bf16[20,4096]{1,0:T(8,128)(2,1)}, u32[]{:S(2)}) copy-start(bf16[20,4096]{1,0:T(8,128)(2,1)} %finish.1) | copy-start | bytes 491524

commit v3 on v2

v3 whole, which is shorter than its diff:
```python
import jax
import jax.numpy as jnp
from jax import lax
from jax.experimental import pallas as pl
from jax.experimental.pallas import tpu as pltpu
from jax.sharding import PartitionSpec as P

RING = 4
WIDTH = 4096
META = 128
ROWS = 40
MESH = pl.DeviceIdType.MESH
ORDERS = (("x", "y", "z"), ("y", "z", "x"), ("z", "x", "y"))
BF = jnp.bfloat16
F32 = jnp.float32


def place():
    dp = lax.axis_index("dp")
    ex = lax.axis_index("expert")
    return {"x": lax.axis_index("sample"), "y": (dp % 2) * 2 + ex // 2, "z": dp // 2}, ex % 2


def device(at, core):
    return {
        "dp": at["z"] * 2 + at["y"] // 2,
        "expert": (at["y"] % 2) * 2 + core,
        "sample": at["x"],
    }


def moved(at, axis, by):
    return {**at, axis: lax.rem(at[axis] + (by + RING), RING)}


def greet(at, core):
    barrier = pltpu.get_barrier_semaphore()
    peers = [device(moved(at, axis, by), core) for axis in "xyz" for by in (1, -1)]
    peers.append(device(at, 1 - core))
    for peer in peers:
        pl.semaphore_signal(barrier, inc=1, device_id=peer, device_id_type=MESH)
    pl.semaphore_wait(barrier, len(peers))


def remote(src, dst, send, recv, peer):
    return pltpu.make_async_remote_copy(
        src_ref=src, dst_ref=dst, send_sem=send, recv_sem=recv, device_id=peer, device_id_type=MESH
    )


class Plan:
    def __init__(self):
        self.now = 0.0
        self.free = {}
        self.ready = {}

    def send(self, key, lane, size):
        rate, delay = (5e5, 1.5) if lane == "pair" else (4.6e4, 2.8)
        end = max(self.now, self.free.get(lane, 0.0)) + size / rate
        self.free[lane] = end
        self.ready[key] = end + delay

    def mark(self, key, delay=0.0):
        self.ready[key] = self.now + delay

    def run(self, actors):
        waiting = [(actor, next(actor, None)) for actor in actors]
        while any(need is not None for _, need in waiting):
            best = None
            for i, (actor, need) in enumerate(waiting):
                if need is None or any(key not in self.ready for key in need[0]):
                    continue
                at = max([self.now] + [self.ready[key] for key in need[0]])
                if best is None or at < best[0]:
                    best = (at, i)
            at, i = best
            actor, need = waiting[i]
            self.now = at + need[1]
            waiting[i] = (actor, next(actor, None))


CHUNK_WIDTHS = (640, 512, 256)
CHUNK_STARTS = (0, 640, 1152)
PART = (WIDTH + META) // 3
GATHER_COPIES = 23
GROUP = RING * ROWS
TOKENS = RING * RING * GROUP
PLANE = RING * GROUP
UNITS = 256
BLOCKS = 6


def turned(a, b):
    return lax.dot_general(a, b, (((1,), (1,)), ((), ())), preferred_element_type=F32)


def gather_kernel(own_ref, wg_ref, wu_ref, wd_ref, out_ref, grad_ref, hidden_ref, *scratch):
    mate, block, total, tiles, weights, info, scales, keep, tsem, wsem, send, recv = scratch
    at, core = place()
    partner = device(at, 1 - core)
    plan = Plan()
    copies = {}
    settled = []
    greet(at, core)
    swap = remote(own_ref.at[1 - core], mate, send.at[9, 0], recv.at[9, 0], partner)
    swap.start()
    swap.wait()

    @pl.when(core == 0)
    def _():
        block[0:20] = own_ref[0]
        block[20:40] = mate[...]

    @pl.when(core == 1)
    def _():
        block[0:20] = mate[...]
        block[20:40] = own_ref[1]

    here = pltpu.make_async_copy(block, out_ref.at[core, at["z"], at["y"], pl.ds(pl.multiple_of(at["x"] * ROWS, 8), ROWS)], keep)
    here.start()

    def columns(s):
        return pl.ds((s % 3) * PART + CHUNK_STARTS[s // 3], CHUNK_WIDTHS[s // 3])

    def view(s, **over):
        to = {**at, **over}
        x = to["x"]
        if isinstance(x, pl.Slice):
            x = pl.ds(x.start * ROWS, x.size * ROWS)
        else:
            x = pl.ds(pl.multiple_of(x * ROWS, 8), ROWS)
        return out_ref.at[core, to["z"], to["y"], x, columns(s)]

    def push(s, k, src, dst, peer, lane, count):
        copy = remote(src, dst, send.at[s, k], recv.at[s, k], peer)
        copy.start()
        copies[s, k] = copy
        plan.send((s, k), lane, count * ROWS * CHUNK_WIDTHS[s // 3] * 2)

    def near(axis, by):
        return device(moved(at, axis, by), core)

    def coord(axis, by):
        return at[axis] if by == 0 else moved(at, axis, by)[axis]

    every = pl.ds(0, RING)
    offset = (0, -1, 1, 2)

    def line(s, l, plane=0):
        d1, d2, d3 = ORDERS[s % 3]
        return view(s, **{d1: every, d2: coord(d2, offset[l]), d3: coord(d3, plane)})

    def hand(s, n):
        d1, d2, d3 = ORDERS[s % 3]
        ref = view(s, **{d1: every, d2: every, d3: coord(d3, offset[n])})
        push(s, 19 + n, ref, ref, partner, "pair", 16)

    def travel(s):
        d1, d2, d3 = ORDERS[s % 3]
        tick = 0.05

        def along(k, ref, axis, by, count):
            push(s, k, ref, ref, near(axis, by), (axis, by), count)

        def spread(l):
            along(7 + 2 * l, line(s, l), d3, 1, 4)
            along(8 + 2 * l, line(s, l), d3, -1, 4)

        mine = block.at[:, columns(s)]
        for k, by in ((0, 1), (1, -1)):
            push(s, k, mine, view(s), near(d1, by), (d1, by), 1)
        yield [(s, 0)], tick
        copies[s, 0].wait_recv()
        along(2, view(s, **{d1: coord(d1, -1)}), d1, 1, 1)
        yield [(s, 1), (s, 2)], tick
        copies[s, 1].wait_recv()
        copies[s, 2].wait_recv()
        if not settled:
            here.wait()
            settled.append(True)
        along(3, line(s, 0), d2, 1, 4)
        along(4, line(s, 0), d2, -1, 4)
        spread(0)
        yield [(s, 3)], tick
        copies[s, 3].wait_recv()
        along(5, view(s, **{d1: pl.ds(0, 2), d2: coord(d2, -1)}), d2, 1, 2)
        spread(1)
        yield [(s, 4)], tick
        copies[s, 4].wait_recv()
        along(6, view(s, **{d1: pl.ds(2, 2), d2: coord(d2, 1)}), d2, -1, 2)
        spread(2)
        yield [(s, 5), (s, 6)], tick
        copies[s, 5].wait_recv()
        copies[s, 6].wait_recv()
        spread(3)
        hand(s, 0)
        for l in range(4):
            for k, by in ((0, 1), (1, -1)):
                yield [(s, 7 + 2 * l + k)], tick
                copies[s, 7 + 2 * l + k].wait_recv()
                if k == l // 2:
                    along(15 + l, line(s, l, -by), d3, by, 4)
        hand(s, 1)
        hand(s, 2)
        yield [(s, 15 + l) for l in range(4)], tick
        for l in range(4):
            copies[s, 15 + l].wait_recv()
        hand(s, 3)
        plan.mark(("all", s))

    def work():
        turn = 0
        for s in range(9):
            w = CHUNK_WIDTHS[s // 3]
            yield [("all", s)] + [(s, 19 + n) for n in range(4)], 0.1
            for n in range(4):
                copies[s, 19 + n].wait_recv()
            lead = META if s == 0 else 0
            loads = []
            start = (s % 3) * PART + CHUNK_STARTS[s // 3] - META + lead
            sources = ((wg_ref, 0), (wu_ref, 0), (wg_ref, 1), (wu_ref, 1), (wd_ref, 0), (wd_ref, 1))
            for k, (ref, j) in enumerate(sources):
                to = weights.at[k, :, pl.ds(lead, w - lead)]
                loads.append(pltpu.make_async_copy(ref.at[j, :, pl.ds(start, w - lead)], to, wsem.at[k]))

            def fetch(half):
                got = []
                for a in range(2):
                    src = out_ref.at[a, pl.ds(2 * half, 2), :, :, columns(s)]
                    got.append(pltpu.make_async_copy(src, tiles.at[half, a, :, :, :, pl.ds(0, w)], tsem.at[half, a]))
                return got

            loads += fetch(0)
            if s == 0:
                loads.append(pltpu.make_async_copy(out_ref.at[0, :, :, :, pl.ds(0, META)], info, keep))
                weights[:, :, :META] = jnp.zeros((BLOCKS, UNITS, META), BF)
            later = fetch(1)
            for copy in loads + later:
                copy.start()
            plan.mark(("load", s), 2.5)
            yield [("load", s)], 4.0 * w / 640
            for half in range(2):
                if half:
                    yield [], 4.0 * w / 640
                for copy in later if half else loads:
                    copy.wait()

                def body(i, carry):
                    z, pair = i // 3, i % 3
                    tile = tiles[half, pair // 2, z, :, :, :w].reshape(PLANE, w)
                    where = pl.ds(pl.multiple_of((2 * half + z) * PLANE, 8), PLANE)
                    for k in range(2):
                        q = pair * 2 + k
                        value = turned(tile, weights[q, :, :w])
                        if s == 0:
                            total[q, where, :] = value
                        else:
                            total[q, where, :] += value
                    return carry

                lax.fori_loop(0, 6, body, 0)

    plan.run([travel(s) for s in range(9)] + [work()])

    first = (2 * lax.axis_index("expert")).astype(F32)
    same = (
        lax.broadcasted_iota(jnp.int32, (GROUP, GROUP), 0) % ROWS
        == lax.broadcasted_iota(jnp.int32, (GROUP, GROUP), 1) % ROWS
    ).astype(F32).astype(BF)

    def scale(i, carry):
        rows = info[i // RING, i % RING]
        meta = rows.astype(F32)
        reward = meta[:, 9:10] * 0.0625
        all_rewards = jnp.dot(same, rows, preferred_element_type=F32)[:, 9:10] * 0.0625
        advantage = reward - (all_rewards - reward) / 3.0
        position = lax.broadcasted_iota(jnp.int32, (GROUP, 1), 0) % 20
        weight = jnp.where(position.astype(F32) < meta[:, 8:9], -advantage, 0.0)
        lane = lax.broadcasted_iota(jnp.int32, (GROUP, 128), 1).astype(F32)
        value = jnp.zeros((GROUP, 128), F32)
        for k in range(2):
            c = 2 + 3 * k
            pair = ((meta[:, c : c + 1] + meta[:, c + 1 : c + 2]) + meta[:, c + 2 : c + 3]) * weight
            value = jnp.where(lane == meta[:, k : k + 1] - first, pair, value)
        scales[pl.ds(pl.multiple_of(i * GROUP, 8), GROUP), :] = value
        return carry

    lax.fori_loop(0, RING * RING, scale, 0)

    def activate(i, carry):
        where = pl.ds(pl.multiple_of(i * 128, 128), 128)
        for j in range(2):
            pre_gate, pre_up = total[2 * j, where, :], total[2 * j + 1, where, :]
            by = scales[where, j : j + 1]
            grad_hidden = total[4 + j, where, :] * by
            prob = 1.0 / (1.0 + jnp.exp(-pre_gate))
            active = pre_gate * prob
            slope = prob * (1.0 + pre_gate * (1.0 - prob))
            grad_ref[where, 2 * j * UNITS : (2 * j + 1) * UNITS] = (grad_hidden * pre_up * slope).astype(BF)
            grad_ref[where, (2 * j + 1) * UNITS : (2 * j + 2) * UNITS] = (grad_hidden * active).astype(BF)
            hidden_ref[where, j * UNITS : (j + 1) * UNITS] = (active * pre_up * by).astype(BF)
        return carry

    lax.fori_loop(0, TOKENS // 128, activate, 0)
    for copy in copies.values():
        copy.wait_send()


def gather_rows(own, w_gate, w_up, w_down):
    anywhere = pl.BlockSpec(memory_space=pl.ANY)
    inside = pl.BlockSpec(memory_space=pltpu.VMEM)
    return pl.pallas_call(
        gather_kernel,
        out_shape=(
            jax.ShapeDtypeStruct((2, RING, RING, GROUP, WIDTH + META), BF),
            jax.ShapeDtypeStruct((TOKENS, 4 * UNITS), BF),
            jax.ShapeDtypeStruct((TOKENS, 2 * UNITS), BF),
        ),
        in_specs=[inside] + [anywhere] * 3,
        out_specs=(anywhere, inside, inside),
        scratch_shapes=[
            pltpu.VMEM((ROWS // 2, WIDTH + META), BF),
            pltpu.VMEM((ROWS, WIDTH + META), BF),
            pltpu.VMEM((BLOCKS, TOKENS, UNITS), F32),
            pltpu.VMEM((2, 2, 2, RING, GROUP, CHUNK_WIDTHS[0]), BF),
            pltpu.VMEM((BLOCKS, UNITS, CHUNK_WIDTHS[0]), BF),
            pltpu.VMEM((RING, RING, GROUP, META), BF),
            pltpu.VMEM((TOKENS, 128), F32),
            pltpu.SemaphoreType.DMA,
            pltpu.SemaphoreType.DMA((2, 2)),
            pltpu.SemaphoreType.DMA((BLOCKS,)),
            pltpu.SemaphoreType.DMA((10, GATHER_COPIES)),
            pltpu.SemaphoreType.DMA((10, GATHER_COPIES)),
        ],
        compiler_params=pltpu.CompilerParams(
            collective_id=0, has_side_effects=True, vmem_limit_bytes=60 * 1024 * 1024
        ),
        name="gather_rows",
    )(own, w_gate, w_up, w_down)


HALF = WIDTH // 2
WIDTHS = (384, 384, 256, 384, 256, 384)
STARTS = (0, 384, 768, 1024, 1408, 1664)
WIDEST = 384
STREAMS = 6
STREAM_COPIES = 22
AHEAD = (3, 1)
BEHIND = (2, 0)


def finish_kernel(grad_ref, hidden_ref, rows_ref, wg_ref, wu_ref, out_ref, dg_ref, du_ref, dd_ref, *scratch):
    n = STREAMS
    acc, mate, fa, ma, pa, fb, mb, pb, fc, mc, pc = [scratch[n * i : n * i + n] for i in range(11)]
    give, weights, done, other_done, across, tiles, made, some, wsem, tsem, msem, hsem, send, recv = scratch[11 * n :]
    plan = Plan()
    at, core = place()
    partner = device(at, 1 - core)
    copies = {}
    every = pl.ds(0, RING)
    offset = (0, -1, 1, 2)

    def near(axis, by):
        return device(moved(at, axis, by), core)

    def coord(axis, by):
        return at[axis] if by == 0 else moved(at, axis, by)[axis]

    def spot(**over):
        to = {**at, **over}
        return to["z"], to["y"], to["x"]

    def order(s):
        return ORDERS[s % 3]

    def push(s, key, k, src, dst, peer, lane, count):
        copy = remote(src, dst, send.at[s, k], recv.at[s, k], peer)
        copy.start()
        copies[(s,) + key] = copy
        plan.send((s,) + key, lane, count * ROWS * WIDTHS[s] * 2)

    def along(s, key, k, src, dst, axis, by, count):
        push(s, key, k, src, dst, near(axis, by), (axis, by), count)

    turns = [(s, far) for c in (0, 3) for far in (True, False) for s in range(c, c + 3)]

    def fetch(turn):
        s, far = turns[turn]
        side = 1 - core if far else core
        columns = pl.ds(pl.multiple_of(side * HALF + STARTS[s], 128), WIDTHS[s])
        got = []
        for q in range(4):
            ref = (wg_ref, wu_ref)[q % 2].at[q // 2, :, columns]
            to = weights.at[turn % 2, q, :, pl.ds(0, WIDTHS[s])]
            got.append(pltpu.make_async_copy(ref, to, wsem.at[turn % 2, q]))
            got[-1].start()
        return got

    fetched = {0: fetch(0)}

    def compute(turn):
        s, far = turns[turn]
        w = WIDTHS[s]
        slot = turn % 2
        if turn + 1 < len(turns):
            fetched[turn + 1] = fetch(turn + 1)
        for copy in fetched[turn]:
            copy.wait()
        if far:
            if s >= 3:
                copies[s - 3, "far"].wait_send()
        else:
            copies[s, "far"].wait_recv()

        def rows_of(z, carry):
            take = pl.ds(pl.multiple_of(z * PLANE, 8), PLANE)
            total = jnp.dot(grad_ref[take, :UNITS], weights[slot, 0, :, :w], preferred_element_type=F32)
            for q in range(1, 4):
                total += jnp.dot(
                    grad_ref[take, q * UNITS : (q + 1) * UNITS], weights[slot, q, :, :w], preferred_element_type=F32
                )
            for i in range(RING * RING):
                y, x = i // RING, i % RING
                piece = total[i * ROWS : (i + 1) * ROWS]
                if far:
                    give[s % 3, z, y, x, :, :w] = piece.astype(BF)
                else:
                    acc[s][z, y, x] = (piece + mate[s][z, y, x].astype(F32)).astype(BF)
            return carry

        lax.fori_loop(0, RING, rows_of, 0)
        if far:
            push(s, ("far",), 21, give.at[s % 3, :, :, :, :, pl.ds(0, w)], mate[s], partner, "pair", 64)
        else:
            plan.mark(("own", s))

    def add(dst, index, *terms):
        total = dst[index].astype(F32)
        for ref, where in terms:
            total = total + ref[where].astype(F32)
        dst[index] = total.astype(BF)

    def line(s, r, by):
        d1, d2, d3 = order(s)
        return acc[s].at[spot(**{d1: every, d2: coord(d2, offset[r]), d3: coord(d3, by)})]

    def add_line(s, r, by, *terms, first=0, count=RING):
        d1, d2, d3 = order(s)

        def body(i, carry):
            where = spot(**{d1: i, d2: coord(d2, offset[r]), d3: coord(d3, by)})
            add(acc[s], where, *[(ref, (r, i) if lead else (i,)) for ref, lead in terms])
            return carry

        lax.fori_loop(first, first + count, body, 0)

    def piece(s, r, half):
        d1, d2, d3 = order(s)
        return acc[s].at[spot(**{d1: pl.ds(2 * half, 2), d2: coord(d2, offset[r])})]

    def half_of(ref, half):
        return ref.at[pl.ds(2 * half, 2)]

    def cell(s, by):
        d1 = order(s)[0]
        return spot(**{d1: coord(d1, by)})

    def travel(s):
        d1, d2, d3 = order(s)
        cost = 0.3
        yield [("own", s)], 0.1
        for r in (3, 2, 1, 0):
            along(s, ("fa", r), r, line(s, r, 2), fa[s].at[r], d3, 1 if r in AHEAD else -1, 4)
        for r in BEHIND:
            along(s, ("ma", r), 4 + r, line(s, r, 1), ma[s].at[r], d3, 1, 4)
        for r in AHEAD:
            along(s, ("pa", r), 8 + r, line(s, r, -1), pa[s].at[r], d3, -1, 4)
        for r in (3, 2, 1, 0):
            yield [(s, "fa", r)], cost
            copies[s, "fa", r].wait_recv()
            if r in AHEAD:
                add_line(s, r, 1, (fa[s], True))
                along(s, ("ma", r), 4 + r, line(s, r, 1), ma[s].at[r], d3, 1, 4)
            else:
                add_line(s, r, -1, (fa[s], True))
                along(s, ("pa", r), 8 + r, line(s, r, -1), pa[s].at[r], d3, -1, 4)
        for r in (3, 2, 1, 0):
            yield [(s, "ma", r), (s, "pa", r)], cost
            copies[s, "ma", r].wait_recv()
            copies[s, "pa", r].wait_recv()
            add_line(s, r, 0, (ma[s], True), (pa[s], True))
            if r == 3:
                along(s, ("fb", 0), 12, piece(s, 3, 0), half_of(fb[s], 0), d2, 1, 2)
                along(s, ("fb", 1), 13, piece(s, 3, 1), half_of(fb[s], 1), d2, -1, 2)
            if r == 2:
                along(s, ("mb", 1), 15, piece(s, 2, 1), half_of(mb[s], 1), d2, 1, 2)
            if r == 1:
                along(s, ("pb", 0), 16, piece(s, 1, 0), half_of(pb[s], 0), d2, -1, 2)
        yield [(s, "fb", 0)], cost
        copies[s, "fb", 0].wait_recv()
        add_line(s, 2, 0, (fb[s], False), first=0, count=2)
        along(s, ("mb", 0), 14, piece(s, 2, 0), half_of(mb[s], 0), d2, 1, 2)
        yield [(s, "fb", 1)], cost
        copies[s, "fb", 1].wait_recv()
        add_line(s, 1, 0, (fb[s], False), first=2, count=2)
        along(s, ("pb", 1), 17, piece(s, 1, 1), half_of(pb[s], 1), d2, -1, 2)
        yield [(s, key, half) for key in ("mb", "pb") for half in (0, 1)], cost
        for half in (0, 1):
            copies[s, "mb", half].wait_recv()
            copies[s, "pb", half].wait_recv()
        add_line(s, 0, 0, (mb[s], False), (pb[s], False))
        along(s, ("fc",), 18, acc[s].at[cell(s, 2)], fc[s], d1, 1, 1)
        along(s, ("pc",), 20, acc[s].at[cell(s, -1)], pc[s], d1, -1, 1)
        yield [(s, "fc")], 0.1
        copies[s, "fc"].wait_recv()
        add(acc[s], cell(s, 1), (fc[s], ...))
        along(s, ("mc",), 19, acc[s].at[cell(s, 1)], mc[s], d1, 1, 1)
        yield [(s, "pc"), (s, "mc")], 0.1
        copies[s, "pc"].wait_recv()
        copies[s, "mc"].wait_recv()
        own = acc[s][cell(s, 0)].astype(F32) + pc[s][...].astype(F32) + mc[s][...].astype(F32)
        done[:, STARTS[s] : STARTS[s] + WIDTHS[s]] = own.astype(BF)
        plan.mark(("end", s))
        yield [("end", s)], 0.0

    def produce():
        for turn, (s, far) in enumerate(turns):
            yield [] if far else [(s, "far")], 3.0 * WIDTHS[s] / 384
            compute(turn)
        plan.mark("produced")

    def weigh():
        yield ["produced"], 0.2

        def load(t):
            got = []
            for a in range(2):
                src = rows_ref.at[a, :, pl.ds(META + t * UNITS, UNITS)]
                got.append(pltpu.make_async_copy(src, tiles.at[t % 2, a], tsem.at[t % 2, a]))
                got[-1].start()
            return got

        loaded = {0: load(0)}
        fetch_hidden = pltpu.make_async_copy(hidden_ref, some, hsem)
        fetch_hidden.start()
        for step in range(2):
            yield [], 5.0 if step == 0 else 2.5
            if step:
                fetch_hidden.wait()

            def turn_over(i, carry):
                where = pl.ds(pl.multiple_of(i * UNITS, UNITS), UNITS)
                for q in range(2 if step else 4):
                    src = (some if step else grad_ref)[where, q * UNITS : (q + 1) * UNITS]
                    across[4 * step + q, :, where] = src.T
                return carry

            lax.fori_loop(0, TOKENS // UNITS, turn_over, 0)
        stored = {}
        for t in range(WIDTH // UNITS):
            yield [], 2.6
            if t + 1 < WIDTH // UNITS:
                loaded[t + 1] = load(t + 1)
            for copy in loaded[t] + stored.pop(t - 2, []):
                copy.wait()

            def body(q, carry):
                value = jnp.dot(across[q], tiles[t % 2, q // 4], preferred_element_type=F32)
                made[t % 2, q] = value.astype(BF)
                return carry

            lax.fori_loop(0, BLOCKS, body, 0)
            stored[t] = []
            for q in range(BLOCKS):
                ref, j = ((dg_ref, du_ref)[q % 2], q // 2) if q < 4 else (dd_ref, q - 4)
                to = ref.at[j, :, pl.ds(t * UNITS, UNITS)]
                stored[t].append(pltpu.make_async_copy(made.at[t % 2, q], to, msem.at[t % 2, q]))
                stored[t][-1].start()
        for some_copies in stored.values():
            for copy in some_copies:
                copy.wait()

    greet(at, core)
    plan.run([travel(s) for s in range(n)] + [produce(), weigh()])
    last = remote(done, other_done, send.at[n, 0], recv.at[n, 0], partner)
    last.start()
    last.wait_recv()

    @pl.when(core == 0)
    def _():
        out_ref[:, :HALF] = done[0:20]
        out_ref[:, HALF:] = other_done[0:20]

    @pl.when(core == 1)
    def _():
        out_ref[:, :HALF] = other_done[20:40]
        out_ref[:, HALF:] = done[20:40]

    last.wait_send()
    for key, copy in copies.items():
        if key[1] != "far" or key[0] >= 3:
            copy.wait_send()


def finish(grads, hidden, rows, w_gate, w_up):
    full = [pltpu.VMEM((RING, RING, RING, ROWS, w), BF) for w in WIDTHS]
    lines = [pltpu.VMEM((RING, RING, ROWS, w), BF) for w in WIDTHS]
    line = [pltpu.VMEM((RING, ROWS, w), BF) for w in WIDTHS]
    cell = [pltpu.VMEM((ROWS, w), BF) for w in WIDTHS]
    anywhere = pl.BlockSpec(memory_space=pl.ANY)
    inside = pl.BlockSpec(memory_space=pltpu.VMEM)
    return pl.pallas_call(
        finish_kernel,
        out_shape=(jax.ShapeDtypeStruct((ROWS // 2, WIDTH), BF),) + (jax.ShapeDtypeStruct(w_gate.shape, BF),) * 3,
        in_specs=[inside] + [anywhere] * 4,
        out_specs=(inside,) + (anywhere,) * 3,
        scratch_shapes=full * 2
        + lines * 3
        + line * 3
        + cell * 3
        + [
            pltpu.VMEM((3, RING, RING, RING, ROWS, WIDEST), BF),
            pltpu.VMEM((2, 4, UNITS, WIDEST), BF),
            pltpu.VMEM((ROWS, HALF), BF),
            pltpu.VMEM((ROWS, HALF), BF),
            pltpu.VMEM((BLOCKS, UNITS, TOKENS), BF),
            pltpu.VMEM((2, 2, TOKENS, UNITS), BF),
            pltpu.VMEM((2, BLOCKS, UNITS, UNITS), BF),
            pltpu.VMEM((TOKENS, 2 * UNITS), BF),
            pltpu.SemaphoreType.DMA((2, 4)),
            pltpu.SemaphoreType.DMA((2, 2)),
            pltpu.SemaphoreType.DMA((2, BLOCKS)),
            pltpu.SemaphoreType.DMA,
            pltpu.SemaphoreType.DMA((STREAMS + 1, STREAM_COPIES)),
            pltpu.SemaphoreType.DMA((STREAMS + 1, STREAM_COPIES)),
        ],
        compiler_params=pltpu.CompilerParams(
            collective_id=1, has_side_effects=True, vmem_limit_bytes=67000000
        ),
        name="finish",
    )(grads, hidden, rows, w_gate, w_up)


def three(values):
    high = lax.reduce_precision(values, 8, 7)
    middle = lax.reduce_precision(values - high, 8, 7)
    return [high, middle, values - high - middle]


def own_rows(tokens, cotangent, routes, gate_weights, lengths, rewards):
    count = tokens.shape[0]
    wide = jnp.ones((count, 1), F32)
    columns = [routes.astype(F32)]
    for k in range(2):
        columns += three(gate_weights[:, k : k + 1])
    columns += [wide * lengths[0, 0].astype(F32), wide * rewards[0, 0].astype(F32)]
    meta = jnp.concatenate(columns, axis=1)
    meta = jnp.pad(meta, ((0, 0), (0, META - meta.shape[1]))).astype(BF)
    return jnp.stack(
        [jnp.concatenate([meta, tokens], axis=1), jnp.concatenate([jnp.zeros_like(meta), cotangent], axis=1)]
    )


def local(tokens, cotangent, routes, gate_weights, lengths, rewards, w_gate, w_up, w_down):
    own = own_rows(tokens, cotangent, routes, gate_weights, lengths, rewards)
    everything, grads, hidden = gather_rows(own, w_gate, w_up, w_down)
    everything = everything.reshape(2, TOKENS, WIDTH + META)
    return finish(grads, hidden, everything, w_gate, w_up)


def solution(mesh):
    rows = P(("dp", "expert", "sample"), None)
    pair = P(("dp", "expert"), "sample")
    weights = P("expert", ("dp", "sample"), None)
    return jax.shard_map(
        local,
        mesh=mesh,
        in_specs=(rows,) * 4 + (pair,) * 2 + (weights,) * 3,
        out_specs=(rows,) + (weights,) * 3,
        check_vma=False,
    )
```

time: 308 us -> 326 us (1.058)
  Pallas kernels: 242 us -> 307 us
  matrix products: 55.3 us -> 0 us
  local copies, waits for them, and re-layouts: 5.3 us -> 14.3 us
    pallas_call x3 -> x2, Pallas kernels: 242 us -> 307 us  [the longest x1 191 us: gather_rows(): pl.pallas_call(gather_kernel, out_shape=(jax.ShapeDtypeStruct((2, RING, R...]
    dot_general x6 -> x0, matrix products: 55.3 us -> none  [the longest x1 11.5 us: local(): forward(g, w_down)]
    unnamed x12 -> x8, local copies, waits for them, and re-layouts: 3 us -> 12.2 us
where the time goes in v3:
time: 326 us; the launch traced here: 325 us
  Pallas kernels  307 us (94%)
  local copies, waits for them, and re-layouts  14.3 us (4%)
    pallas_call x1, Pallas kernels, gather_rows(): pl.pallas_call(gather_kernel, out_shape=(jax.ShapeDtypeStruct((2, RING, R...  191 us
    pallas_call x1, Pallas kernels, finish(): pl.pallas_call(finish_kernel, out_shape=(jax.ShapeDtypeStruct((ROWS // 2,...  116 us
    unnamed x8, local copies, waits for them, and re-layouts  12.2 us

profile of v3, /device:TPU:1, one launch (start us, length us, event | category | flops | bytes accessed | tf_op | source)
XLA Modules:
  0.0 325.4 jit_solution(7225263425201235264)
XLA Ops:
  1.9 0.7 convert_convert_fusion
  2.6 0.8 fusion.5
  3.4 0.1 copy.22
  3.5 0.1 copy.20
  3.6 0.1 copy.18
  3.7 0.1 concatenate.10
  3.8 0.9 fusion.2
  4.8 0.9 pad_bitcast_fusion
  5.7 0.8 pad_maximum_fusion.own_ref
  6.5 190.6 %gather_rows.1 = (bf16[2,4,4,160,4224]{4,3,2,1,0:T(8,128)(2,1)}, bf16[2560,1024]{1,0:T(8,128)(2,1)}, bf16[2560,512]{1,0:T(8,128)(2,1)}) custom-call(bf16[2,20,4224]{2,1,0:T(8,128)(2,1)} %pad_maximum_fusion.own_ref, bf16[2,256,4096]{2,1,0:T(8,128)(2,1)} %wg_ref.3, bf16[2,256,4096]{2,1,0:T(8,128)(2,1)} %wu_ref.3, bf16[2,256,4096]{2,1,0:T(8,128)(2,1)} %wd_ref.1), custom_call_target="tpu_custom_call" | custom-call | tf_op jit(solution)/shard_map/gather_rows/pallas_call | solution.py:312
  197.1 116.1 %finish.1 = (bf16[20,4096]{1,0:T(8,128)(2,1)}, bf16[2,256,4096]{2,1,0:T(8,128)(2,1)}, bf16[2,256,4096]{2,1,0:T(8,128)(2,1)}, bf16[2,256,4096]{2,1,0:T(8,128)(2,1)}) custom-call(bf16[2560,1024]{1,0:T(8,128)(2,1)} %get-tuple-element.7.grad_ref, bf16[2560,512]{1,0:T(8,128)(2,1)} %get-tuple-element.8.hidden_ref, bf16[2,2560,4224]{2,1,0:T(8,128)(2,1)} %bitcast.7, ...), custom_call_target="tpu_custom_call" | custom-call | tf_op jit(solution)/shard_map/finish/pallas_call | solution.py:612
  313.2 1.6 copy.29
  314.9 0.0 copy-start.1
  314.9 4.8 %copy.30 = bf16[2,256,4096]{2,1,0:T(8,128)(2,1)} copy(bf16[2,256,4096]{2,1,0:T(8,128)(2,1)} %get-tuple-element.26) | data formatting | bytes 8388608
  319.7 0.0 copy-done.1
  319.7 0.0 copy-start
  319.7 2.1 copy.31
  321.8 1.6 copy-done
  323.4 2.0 copy.32
  (3 shorter events, 0.0 us)
Async XLA Ops:
  314.9 4.9 %copy-start.1 = (bf16[2,256,4096]{2,1,0:T(8,128)(2,1)S(1)}, bf16[2,256,4096]{2,1,0:T(8,128)(2,1)}, u32[]{:S(2)}) copy-start(bf16[2,256,4096]{2,1,0:T(8,128)(2,1)} %get-tuple-element.27) | copy-start | bytes 12582916
  319.7 3.7 %copy-start = (bf16[2,256,4096]{2,1,0:T(8,128)(2,1)S(1)}, bf16[2,256,4096]{2,1,0:T(8,128)(2,1)}, u32[]{:S(2)}) copy-start(bf16[2,256,4096]{2,1,0:T(8,128)(2,1)} %get-tuple-element.28) | copy-start | bytes 12582916

commit v4 on v3

--- a/solution.py
+++ b/solution.py
@@ -49,13 +49,15 @@
 
 
 class Plan:
-    def __init__(self):
+    def __init__(self, delay, slack):
+        self.delay = delay
+        self.slack = slack
         self.now = 0.0
         self.free = {}
         self.ready = {}
 
     def send(self, key, lane, size):
-        rate, delay = (5e5, 1.5) if lane == "pair" else (4.6e4, 2.8)
+        rate, delay = (5e5, 1.5) if lane == "pair" else (4.6e4, self.delay)
         end = max(self.now, self.free.get(lane, 0.0)) + size / rate
         self.free[lane] = end
         self.ready[key] = end + delay
@@ -70,7 +72,8 @@
             for i, (actor, need) in enumerate(waiting):
                 if need is None or any(key not in self.ready for key in need[0]):
                     continue
-                at = max([self.now] + [self.ready[key] for key in need[0]])
+                queued = [self.free.get(lane, 0.0) - self.slack for lane in need[2:]]
+                at = max([self.now] + [self.ready[key] for key in need[0]] + queued)
                 if best is None or at < best[0]:
                     best = (at, i)
             at, i = best
@@ -79,8 +82,8 @@
             waiting[i] = (actor, next(actor, None))
 
 
-CHUNK_WIDTHS = (640, 512, 256)
-CHUNK_STARTS = (0, 640, 1152)
+CHUNK_WIDTHS = (512, 640, 256)
+CHUNK_STARTS = (0, 512, 1152)
 PART = (WIDTH + META) // 3
 GATHER_COPIES = 23
 GROUP = RING * ROWS
@@ -98,7 +101,7 @@
     mate, block, total, tiles, weights, info, scales, keep, tsem, wsem, send, recv = scratch
     at, core = place()
     partner = device(at, 1 - core)
-    plan = Plan()
+    plan = Plan(3.4, 5.0)
     copies = {}
     settled = []
     greet(at, core)
@@ -169,10 +172,11 @@
         mine = block.at[:, columns(s)]
         for k, by in ((0, 1), (1, -1)):
             push(s, k, mine, view(s), near(d1, by), (d1, by), 1)
-        yield [(s, 0)], tick
+        ahead = lambda *axes: [(axis, by) for axis in axes for by in (1, -1)] if s >= 3 else []
+        yield [(s, 0)], tick, *ahead(d1)
         copies[s, 0].wait_recv()
         along(2, view(s, **{d1: coord(d1, -1)}), d1, 1, 1)
-        yield [(s, 1), (s, 2)], tick
+        yield [(s, 1), (s, 2)], tick, *ahead(d2)
         copies[s, 1].wait_recv()
         copies[s, 2].wait_recv()
         if not settled:
@@ -180,15 +184,17 @@
             settled.append(True)
         along(3, line(s, 0), d2, 1, 4)
         along(4, line(s, 0), d2, -1, 4)
+        yield [], tick, (d3, 1), (d3, -1)
         spread(0)
         yield [(s, 3)], tick
         copies[s, 3].wait_recv()
         along(5, view(s, **{d1: pl.ds(0, 2), d2: coord(d2, -1)}), d2, 1, 2)
-        spread(1)
         yield [(s, 4)], tick
         copies[s, 4].wait_recv()
         along(6, view(s, **{d1: pl.ds(2, 2), d2: coord(d2, 1)}), d2, -1, 2)
-        spread(2)
+        for l in (1, 2):
+            yield [], tick, (d3, 1), (d3, -1)
+            spread(l)
         yield [(s, 5), (s, 6)], tick
         copies[s, 5].wait_recv()
         copies[s, 6].wait_recv()
@@ -208,60 +214,6 @@
         hand(s, 3)
         plan.mark(("all", s))
 
-    def work():
-        turn = 0
-        for s in range(9):
-            w = CHUNK_WIDTHS[s // 3]
-            yield [("all", s)] + [(s, 19 + n) for n in range(4)], 0.1
-            for n in range(4):
-                copies[s, 19 + n].wait_recv()
-            lead = META if s == 0 else 0
-            loads = []
-            start = (s % 3) * PART + CHUNK_STARTS[s // 3] - META + lead
-            sources = ((wg_ref, 0), (wu_ref, 0), (wg_ref, 1), (wu_ref, 1), (wd_ref, 0), (wd_ref, 1))
-            for k, (ref, j) in enumerate(sources):
-                to = weights.at[k, :, pl.ds(lead, w - lead)]
-                loads.append(pltpu.make_async_copy(ref.at[j, :, pl.ds(start, w - lead)], to, wsem.at[k]))
-
-            def fetch(half):
-                got = []
-                for a in range(2):
-                    src = out_ref.at[a, pl.ds(2 * half, 2), :, :, columns(s)]
-                    got.append(pltpu.make_async_copy(src, tiles.at[half, a, :, :, :, pl.ds(0, w)], tsem.at[half, a]))
-                return got
-
-            loads += fetch(0)
-            if s == 0:
-                loads.append(pltpu.make_async_copy(out_ref.at[0, :, :, :, pl.ds(0, META)], info, keep))
-                weights[:, :, :META] = jnp.zeros((BLOCKS, UNITS, META), BF)
-            later = fetch(1)
-            for copy in loads + later:
-                copy.start()
-            plan.mark(("load", s), 2.5)
-            yield [("load", s)], 4.0 * w / 640
-            for half in range(2):
-                if half:
-                    yield [], 4.0 * w / 640
-                for copy in later if half else loads:
-                    copy.wait()
-
-                def body(i, carry):
-                    z, pair = i // 3, i % 3
-                    tile = tiles[half, pair // 2, z, :, :, :w].reshape(PLANE, w)
-                    where = pl.ds(pl.multiple_of((2 * half + z) * PLANE, 8), PLANE)
-                    for k in range(2):
-                        q = pair * 2 + k
-                        value = turned(tile, weights[q, :, :w])
-                        if s == 0:
-                            total[q, where, :] = value
-                        else:
-                            total[q, where, :] += value
-                    return carry
-
-                lax.fori_loop(0, 6, body, 0)
-
-    plan.run([travel(s) for s in range(9)] + [work()])
-
     first = (2 * lax.axis_index("expert")).astype(F32)
     same = (
         lax.broadcasted_iota(jnp.int32, (GROUP, GROUP), 0) % ROWS
@@ -285,7 +237,70 @@
         scales[pl.ds(pl.multiple_of(i * GROUP, 8), GROUP), :] = value
         return carry
 
-    lax.fori_loop(0, RING * RING, scale, 0)
+    pending = {}
+
+    def needs(s):
+        return [("all", s)] + [(s, 19 + n) for n in range(4)]
+
+    def begin(s):
+        w = CHUNK_WIDTHS[s // 3]
+        for n in range(4):
+            copies[s, 19 + n].wait_recv()
+        lead = META if s == 0 else 0
+        start = (s % 3) * PART + CHUNK_STARTS[s // 3] - META + lead
+        slot = s % 2
+        loads = [[], []]
+        sources = ((wg_ref, 0), (wu_ref, 0), (wg_ref, 1), (wu_ref, 1), (wd_ref, 0), (wd_ref, 1))
+        for k, (ref, j) in enumerate(sources):
+            to = weights.at[slot, k, :, pl.ds(lead, w - lead)]
+            loads[0].append(pltpu.make_async_copy(ref.at[j, :, pl.ds(start, w - lead)], to, wsem.at[slot, k]))
+        for half in range(2):
+            for a in range(2):
+                src = out_ref.at[a, pl.ds(2 * half, 2), :, :, columns(s)]
+                to = tiles.at[slot, half, a, :, :, :, pl.ds(0, w)]
+                loads[half].append(pltpu.make_async_copy(src, to, tsem.at[slot, half, a]))
+        if s == 0:
+            loads[0].append(pltpu.make_async_copy(out_ref.at[0, :, :, :, pl.ds(0, META)], info, keep))
+            weights[0, :, :, :META] = jnp.zeros((BLOCKS, UNITS, META), BF)
+        for half in range(2):
+            for copy in loads[half]:
+                copy.start()
+        pending[s] = loads
+        plan.mark(("load", s), 2.5)
+
+    def work():
+        for s in range(9):
+            w = CHUNK_WIDTHS[s // 3]
+            cost = {640: 2.7, 512: 2.2, 384: 2.0, 256: 1.7}[w]
+            if s not in pending:
+                yield needs(s), 0.1
+                begin(s)
+            for half in range(2):
+                yield [("load", s)], cost
+                for copy in pending[s][half]:
+                    copy.wait()
+
+                def body(i, carry):
+                    z, pair = i // 3, i % 3
+                    tile = tiles[s % 2, half, pair // 2, z, :, :, :w].reshape(PLANE, w)
+                    where = pl.ds(pl.multiple_of((2 * half + z) * PLANE, 8), PLANE)
+                    for k in range(2):
+                        q = pair * 2 + k
+                        value = turned(tile, weights[s % 2, q, :, :w])
+                        if s == 0:
+                            total[q, where, :] = value
+                        else:
+                            total[q, where, :] += value
+                    return carry
+
+                lax.fori_loop(0, 6, body, 0)
+                if half == 0 and s < 8 and all(plan.ready.get(key, 1e9) <= plan.now for key in needs(s + 1)):
+                    begin(s + 1)
+            if s == 0:
+                yield [], 4.2
+                lax.fori_loop(0, RING * RING, scale, 0)
+
+    plan.run([travel(s) for s in range(9)] + [work()])
 
     def activate(i, carry):
         where = pl.ds(pl.multiple_of(i * 128, 128), 128)
@@ -322,13 +337,13 @@
             pltpu.VMEM((ROWS // 2, WIDTH + META), BF),
             pltpu.VMEM((ROWS, WIDTH + META), BF),
             pltpu.VMEM((BLOCKS, TOKENS, UNITS), F32),
-            pltpu.VMEM((2, 2, 2, RING, GROUP, CHUNK_WIDTHS[0]), BF),
-            pltpu.VMEM((BLOCKS, UNITS, CHUNK_WIDTHS[0]), BF),
+            pltpu.VMEM((2, 2, 2, 2, RING, GROUP, max(CHUNK_WIDTHS)), BF),
+            pltpu.VMEM((2, BLOCKS, UNITS, max(CHUNK_WIDTHS)), BF),
             pltpu.VMEM((RING, RING, GROUP, META), BF),
             pltpu.VMEM((TOKENS, 128), F32),
             pltpu.SemaphoreType.DMA,
-            pltpu.SemaphoreType.DMA((2, 2)),
-            pltpu.SemaphoreType.DMA((BLOCKS,)),
+            pltpu.SemaphoreType.DMA((2, 2, 2)),
+            pltpu.SemaphoreType.DMA((2, BLOCKS)),
             pltpu.SemaphoreType.DMA((10, GATHER_COPIES)),
             pltpu.SemaphoreType.DMA((10, GATHER_COPIES)),
         ],
@@ -353,7 +368,7 @@
     n = STREAMS
     acc, mate, fa, ma, pa, fb, mb, pb, fc, mc, pc = [scratch[n * i : n * i + n] for i in range(11)]
     give, weights, done, other_done, across, tiles, made, some, wsem, tsem, msem, hsem, send, recv = scratch[11 * n :]
-    plan = Plan()
+    plan = Plan(5.0, 9.0)
     at, core = place()
     partner = device(at, 1 - core)
     copies = {}
@@ -467,14 +482,16 @@
 
     def travel(s):
         d1, d2, d3 = order(s)
-        cost = 0.3
+        cost = 0.25
         yield [("own", s)], 0.1
-        for r in (3, 2, 1, 0):
-            along(s, ("fa", r), r, line(s, r, 2), fa[s].at[r], d3, 1 if r in AHEAD else -1, 4)
-        for r in BEHIND:
-            along(s, ("ma", r), 4 + r, line(s, r, 1), ma[s].at[r], d3, 1, 4)
-        for r in AHEAD:
-            along(s, ("pa", r), 8 + r, line(s, r, -1), pa[s].at[r], d3, -1, 4)
+        for up, down in ((3, 2), (1, 0)):
+            yield [], 0.05, (d3, 1), (d3, -1)
+            along(s, ("fa", up), up, line(s, up, 2), fa[s].at[up], d3, 1, 4)
+            along(s, ("fa", down), down, line(s, down, 2), fa[s].at[down], d3, -1, 4)
+        for up, down in ((2, 3), (0, 1)):
+            yield [], 0.05, (d3, 1), (d3, -1)
+            along(s, ("ma", up), 4 + up, line(s, up, 1), ma[s].at[up], d3, 1, 4)
+            along(s, ("pa", down), 8 + down, line(s, down, -1), pa[s].at[down], d3, -1, 4)
         for r in (3, 2, 1, 0):
             yield [(s, "fa", r)], cost
             copies[s, "fa", r].wait_recv()
@@ -525,7 +542,7 @@
 
     def produce():
         for turn, (s, far) in enumerate(turns):
-            yield [] if far else [(s, "far")], 3.0 * WIDTHS[s] / 384
+            yield [] if far else [(s, "far")], (1.9 if far else 2.8) * WIDTHS[s] / 384
             compute(turn)
         plan.mark("produced")
 
@@ -544,7 +561,7 @@
         fetch_hidden = pltpu.make_async_copy(hidden_ref, some, hsem)
         fetch_hidden.start()
         for step in range(2):
-            yield [], 5.0 if step == 0 else 2.5
+            yield [], 2.2 if step == 0 else 1.2
             if step:
                 fetch_hidden.wait()
 
@@ -558,7 +575,7 @@
             lax.fori_loop(0, TOKENS // UNITS, turn_over, 0)
         stored = {}
         for t in range(WIDTH // UNITS):
-            yield [], 2.6
+            yield [], 2.0
             if t + 1 < WIDTH // UNITS:
                 loaded[t + 1] = load(t + 1)
             for copy in loaded[t] + stored.pop(t - 2, []):

time: 326 us -> 271 us (0.83)
  Pallas kernels: 307 us -> 252 us
    pallas_call x1, Pallas kernels: 191 us -> 145 us  [gather_rows(): pl.pallas_call(gather_kernel, out_shape=(jax.ShapeDtypeStruct((2, RING, R...]
    pallas_call x1, Pallas kernels: 116 us -> 107 us  [finish(): pl.pallas_call(finish_kernel, out_shape=(jax.ShapeDtypeStruct((ROWS // 2,...]
where the time goes in v4:
time: 271 us
  Pallas kernels  252 us (93%)
  local copies, waits for them, and re-layouts  14.3 us (5%)
    pallas_call x1, Pallas kernels, gather_rows(): pl.pallas_call(gather_kernel, out_shape=(jax.ShapeDtypeStruct((2, RING, R...  145 us
    pallas_call x1, Pallas kernels, finish(): pl.pallas_call(finish_kernel, out_shape=(jax.ShapeDtypeStruct((ROWS // 2,...  107 us
    unnamed x8, local copies, waits for them, and re-layouts  12.2 us

profile of v4, /device:TPU:1, one launch (start us, length us, event | category | flops | bytes accessed | tf_op | source)
XLA Modules:
  0.0 270.8 jit_solution(7469952364546860316)
XLA Ops:
  1.9 0.7 convert_convert_fusion
  2.6 0.8 fusion.5
  3.4 0.1 copy.22
  3.5 0.1 copy.20
  3.6 0.1 copy.18
  3.7 0.1 concatenate.10
  3.8 0.9 fusion.2
  4.8 0.9 pad_bitcast_fusion
  5.7 0.8 pad_maximum_fusion.own_ref
  6.5 145.3 %gather_rows.1 = (bf16[2,4,4,160,4224]{4,3,2,1,0:T(8,128)(2,1)}, bf16[2560,1024]{1,0:T(8,128)(2,1)}, bf16[2560,512]{1,0:T(8,128)(2,1)}) custom-call(bf16[2,20,4224]{2,1,0:T(8,128)(2,1)} %pad_maximum_fusion.own_ref, bf16[2,256,4096]{2,1,0:T(8,128)(2,1)} %wg_ref.3, bf16[2,256,4096]{2,1,0:T(8,128)(2,1)} %wu_ref.3, bf16[2,256,4096]{2,1,0:T(8,128)(2,1)} %wd_ref.1), custom_call_target="tpu_custom_call" | custom-call | tf_op jit(solution)/shard_map/gather_rows/pallas_call | solution.py:327
  151.8 106.8 %finish.1 = (bf16[20,4096]{1,0:T(8,128)(2,1)}, bf16[2,256,4096]{2,1,0:T(8,128)(2,1)}, bf16[2,256,4096]{2,1,0:T(8,128)(2,1)}, bf16[2,256,4096]{2,1,0:T(8,128)(2,1)}) custom-call(bf16[2560,1024]{1,0:T(8,128)(2,1)} %get-tuple-element.7.grad_ref, bf16[2560,512]{1,0:T(8,128)(2,1)} %get-tuple-element.8.hidden_ref, bf16[2,2560,4224]{2,1,0:T(8,128)(2,1)} %bitcast.7, ...), custom_call_target="tpu_custom_call" | custom-call | tf_op jit(solution)/shard_map/finish/pallas_call | solution.py:629
  258.6 1.6 copy.29
  260.2 0.0 copy-start.1
  260.2 4.8 %copy.30 = bf16[2,256,4096]{2,1,0:T(8,128)(2,1)} copy(bf16[2,256,4096]{2,1,0:T(8,128)(2,1)} %get-tuple-element.26) | data formatting | bytes 8388608
  265.0 0.0 copy-done.1
  265.1 0.0 copy-start
  265.1 2.1 copy.31
  267.2 1.6 copy-done
  268.8 2.0 copy.32
  (3 shorter events, 0.0 us)
Async XLA Ops:
  260.2 4.9 %copy-start.1 = (bf16[2,256,4096]{2,1,0:T(8,128)(2,1)S(1)}, bf16[2,256,4096]{2,1,0:T(8,128)(2,1)}, u32[]{:S(2)}) copy-start(bf16[2,256,4096]{2,1,0:T(8,128)(2,1)} %get-tuple-element.27) | copy-start | bytes 12582916
  265.1 3.7 %copy-start = (bf16[2,256,4096]{2,1,0:T(8,128)(2,1)S(1)}, bf16[2,256,4096]{2,1,0:T(8,128)(2,1)}, u32[]{:S(2)}) copy-start(bf16[2,256,4096]{2,1,0:T(8,128)(2,1)} %get-tuple-element.28) | copy-start | bytes 12582916

commit v5 on v4

--- a/solution.py
+++ b/solution.py
@@ -82,8 +82,8 @@
             waiting[i] = (actor, next(actor, None))
 
 
-CHUNK_WIDTHS = (512, 640, 256)
-CHUNK_STARTS = (0, 512, 1152)
+CHUNK_WIDTHS = (256, 640, 512)
+CHUNK_STARTS = (0, 256, 896)
 PART = (WIDTH + META) // 3
 GATHER_COPIES = 23
 GROUP = RING * ROWS

time: 271 us -> 269 us (level)
  Pallas kernels: 252 us -> 249 us
where the time goes in v5:
time: 269 us; the launch traced here: 268 us
  Pallas kernels  249 us (93%)
  local copies, waits for them, and re-layouts  14.3 us (5%)
    pallas_call x1, Pallas kernels, gather_rows(): pl.pallas_call(gather_kernel, out_shape=(jax.ShapeDtypeStruct((2, RING, R...  144 us
    pallas_call x1, Pallas kernels, finish(): pl.pallas_call(finish_kernel, out_shape=(jax.ShapeDtypeStruct((ROWS // 2,...  106 us
    unnamed x8, local copies, waits for them, and re-layouts  12.2 us

profile of v5, /device:TPU:1, one launch (start us, length us, event | category | flops | bytes accessed | tf_op | source)
XLA Modules:
  0.0 268.2 jit_solution(5037903022544407356)
XLA Ops:
  1.9 0.7 convert_convert_fusion
  2.6 0.8 fusion.5
  3.4 0.1 copy.22
  3.5 0.1 copy.20
  3.6 0.1 copy.18
  3.7 0.1 concatenate.10
  3.8 0.9 fusion.2
  4.8 0.9 pad_bitcast_fusion
  5.7 0.8 pad_maximum_fusion.own_ref
  6.5 143.5 %gather_rows.1 = (bf16[2,4,4,160,4224]{4,3,2,1,0:T(8,128)(2,1)}, bf16[2560,1024]{1,0:T(8,128)(2,1)}, bf16[2560,512]{1,0:T(8,128)(2,1)}) custom-call(bf16[2,20,4224]{2,1,0:T(8,128)(2,1)} %pad_maximum_fusion.own_ref, bf16[2,256,4096]{2,1,0:T(8,128)(2,1)} %wg_ref.3, bf16[2,256,4096]{2,1,0:T(8,128)(2,1)} %wu_ref.3, bf16[2,256,4096]{2,1,0:T(8,128)(2,1)} %wd_ref.1), custom_call_target="tpu_custom_call" | custom-call | tf_op jit(solution)/shard_map/gather_rows/pallas_call | solution.py:327
  150.1 105.9 %finish.1 = (bf16[20,4096]{1,0:T(8,128)(2,1)}, bf16[2,256,4096]{2,1,0:T(8,128)(2,1)}, bf16[2,256,4096]{2,1,0:T(8,128)(2,1)}, bf16[2,256,4096]{2,1,0:T(8,128)(2,1)}) custom-call(bf16[2560,1024]{1,0:T(8,128)(2,1)} %get-tuple-element.7.grad_ref, bf16[2560,512]{1,0:T(8,128)(2,1)} %get-tuple-element.8.hidden_ref, bf16[2,2560,4224]{2,1,0:T(8,128)(2,1)} %bitcast.7, ...), custom_call_target="tpu_custom_call" | custom-call | tf_op jit(solution)/shard_map/finish/pallas_call | solution.py:629
  256.0 1.6 copy.29
  257.6 0.0 copy-start.1
  257.6 4.8 %copy.30 = bf16[2,256,4096]{2,1,0:T(8,128)(2,1)} copy(bf16[2,256,4096]{2,1,0:T(8,128)(2,1)} %get-tuple-element.26) | data formatting | bytes 8388608
  262.4 0.0 copy-done.1
  262.4 0.0 copy-start
  262.4 2.1 copy.31
  264.6 1.6 copy-done
  266.1 2.0 copy.32
  (3 shorter events, 0.0 us)
Async XLA Ops:
  257.6 4.9 %copy-start.1 = (bf16[2,256,4096]{2,1,0:T(8,128)(2,1)S(1)}, bf16[2,256,4096]{2,1,0:T(8,128)(2,1)}, u32[]{:S(2)}) copy-start(bf16[2,256,4096]{2,1,0:T(8,128)(2,1)} %get-tuple-element.27) | copy-start | bytes 12582916
  262.4 3.7 %copy-start = (bf16[2,256,4096]{2,1,0:T(8,128)(2,1)S(1)}, bf16[2,256,4096]{2,1,0:T(8,128)(2,1)}, u32[]{:S(2)}) copy-start(bf16[2,256,4096]{2,1,0:T(8,128)(2,1)} %get-tuple-element.28) | copy-start | bytes 12582916
